TPU v7x, 32 devices: a whole 2x2x4 slice. The times are simulated.
32 devices in a mesh: section: 2 (over y), dp: 4 (over x, core), mp: 4 (over z).
Axes of the slice: x: 2, y: 2, z: 4, core: 2. Of those that a mesh axis runs over, the one named last changes fastest.
Arguments:
- block_input: bfloat16 [2, 4, 1024, 2048], P(None, 'dp', 'mp'), may hold values from -6 to 6
- out_grad: bfloat16 [2, 4, 1024, 2048], P(None, 'dp', 'mp'), may hold values from -6 to 6
- lengths: int32 [2, 4], P(None, 'dp'), may hold values from 1 to 1024, 3072 in all within a row
- norm_gain: float32 [2, 2048], P('section'), may hold values from 0.1 to 1.9
- in_weight: bfloat16 [2, 2048, 2, 4096], P('section', None, None, 'mp'), may hold values from -0.125 to 0.125
- state_weight: bfloat16 [2, 2048, 256], P('section'), may hold values from -0.125 to 0.125
- step_weight: bfloat16 [2, 2048, 64], P('section', None, 'mp'), may hold values from -0.125 to 0.125
- conv_inner: float32 [2, 4, 4096], P('section', None, 'mp'), may hold values from -0.6 to 0.6
- conv_state: float32 [2, 4, 256], P('section'), may hold values from -0.6 to 0.6
- step_bias: float32 [2, 64], P('section', 'mp'), may hold values from -9 to -2
- decay_log: float32 [2, 64], P('section', 'mp'), may hold values from 0 to 2.77
- skip_gain: float32 [2, 64], P('section', 'mp'), may hold values from 0.25 to 2
- gate_gain: float32 [2, 4096], P('section', 'mp'), may hold values from 0.1 to 1.9
- out_weight: bfloat16 [2, 4096, 2048], P('section', 'mp'), may hold values from -0.09375 to 0.09375
Outputs:
- section_out: bfloat16 [2, 2, 4, 1024, 2048], P('section', None, 'dp', 'mp')
- section_in_grad: float32 [2, 2, 4, 1024, 2048], P('section', None, 'dp', 'mp')
- grad_norm_gain: float32 [2, 2048], P('section')
- grad_in_weight: float32 [2, 2048, 2, 4096], P('section', None, None, 'mp')
- grad_state_weight: float32 [2, 2048, 256], P('section')
- grad_step_weight: float32 [2, 2048, 64], P('section', None, 'mp')
- grad_conv_inner: float32 [2, 4, 4096], P('section', None, 'mp')
- grad_conv_state: float32 [2, 4, 256], P('section')
- grad_step_bias: float32 [2, 64], P('section', 'mp')
- grad_decay_log: float32 [2, 64], P('section', 'mp')
- grad_skip_gain: float32 [2, 64], P('section', 'mp')
- grad_gate_gain: float32 [2, 4096], P('section', 'mp')
- grad_out_weight: float32 [2, 4096, 2048], P('section', 'mp')
Inputs may be any that keep to these rules, and one draw needn't show every extreme that they name: Each micro-batch's lengths sum to 3072, and the longest of each micro-batch is 1024.
All inputs are finite; a program needn't handle non-finite values. No bound on the sum of `lengths` on one device may be relied on, other than what follows from the above.
Results may differ from a plain program's by a relative error of at most 0.012.
The roundings to bfloat16 on the way count: a program that leaves them out, or rounds other values in their place, can miss the bound.
Values may be sent and summed in bfloat16 or wider, within the bound.
A program may use at most 320 MiB of HBM per device.

v0:
```python
import jax
import jax.numpy as jnp
from jax import lax
from jax.sharding import PartitionSpec as P

BLOCK_LEN = 256


epsilon = 1e-05
highest = lax.Precision.HIGHEST


def shifted(value, axis, by):
    length = lax.axis_size(axis)
    pairs = [(i, i + by) for i in range(length) if 0 <= i + by < length]
    return lax.ppermute(value, axis, pairs)


def causal_conv(series, kernel):
    taps = kernel.shape[0]
    length = series.shape[0]
    padded = jnp.concatenate([jnp.zeros((taps - 1, series.shape[1]), jnp.float32), series], axis=0)
    summed = jnp.zeros_like(series)
    for offset in range(taps):
        summed = summed + kernel[offset] * padded[offset : offset + length]
    return summed


def state_scan(head_inputs, b_matrix, c_matrix, step_size, decay_rates, skip_gain):
    length, head_count, head_width = head_inputs.shape
    block_count = length // BLOCK_LEN
    x_blocks = head_inputs.reshape(block_count, BLOCK_LEN, head_count, head_width)
    b_blocks = b_matrix.reshape(block_count, BLOCK_LEN, -1)
    c_blocks = c_matrix.reshape(block_count, BLOCK_LEN, -1)
    step_blocks = step_size.reshape(block_count, BLOCK_LEN, head_count)
    log_decay = -jnp.cumsum(step_blocks * decay_rates, axis=1)
    scores = jnp.einsum("ktn,ksn->kts", c_blocks, b_blocks, precision=highest)
    ahead = jnp.arange(BLOCK_LEN)[:, None] >= jnp.arange(BLOCK_LEN)[None, :]
    causal = ahead[None, :, :, None]
    log_gap = log_decay[:, :, None, :] - log_decay[:, None, :, :]
    weights = jnp.where(causal, jnp.exp(jnp.where(causal, log_gap, 0.0)), 0.0)
    weights = weights * scores[:, :, :, None] * step_blocks[:, None, :, :]
    within = jnp.einsum("ktsh,kshp->kthp", weights, x_blocks, precision=highest)
    tail_decay = jnp.exp(log_decay[:, -1:, :] - log_decay) * step_blocks
    states = jnp.einsum(
        "ksn,kshp->khnp", b_blocks, x_blocks * tail_decay[:, :, :, None], precision=highest
    )
    carried = jnp.zeros(states.shape[1:], jnp.float32)
    entering = []
    for block_index in range(block_count):
        entering.append(carried)
        carried = jnp.exp(log_decay[block_index, -1])[:, None, None] * carried + states[block_index]
    entering = jnp.stack(entering)
    cross = (
        jnp.einsum("ktn,khnp->kthp", c_blocks, entering, precision=highest)
        * jnp.exp(log_decay)[:, :, :, None]
    )
    result = within + cross + skip_gain[None, None, :, None] * x_blocks
    return result.reshape(length, head_count, head_width)


def round_trip(values):
    return lax.optimization_barrier(values.astype(jnp.bfloat16)).astype(jnp.float32)


def conv_front(inner_pre, state_pre, conv_inner, conv_state):
    return (
        jax.nn.silu(causal_conv(inner_pre, conv_inner)),
        jax.nn.silu(causal_conv(state_pre, conv_state)),
    )


def mixer_core(gate_pre, inner_act, state_act, step_pre, step_bias, decay_log, skip_gain):
    length, inner_width = inner_act.shape
    head_count = step_bias.shape[0]
    state_width = state_act.shape[1] // 2
    step_size = jax.nn.softplus(step_pre + step_bias)
    mixed = state_scan(
        inner_act.reshape(length, head_count, inner_width // head_count),
        state_act[:, :state_width],
        state_act[:, state_width:],
        step_size,
        jnp.exp(decay_log),
        skip_gain,
    )
    return mixed.reshape(length, inner_width) * jax.nn.silu(gate_pre)


def on_device(
    block_input,
    out_grad,
    lengths,
    norm_gain,
    in_weight,
    state_weight,
    step_weight,
    conv_inner,
    conv_state,
    step_bias,
    decay_log,
    skip_gain,
    gate_gain,
    out_weight,
):
    section_id = lax.axis_index("section")
    part_count = lax.axis_size("mp")
    part_index = lax.axis_index("mp")
    micro_count = block_input.shape[0]
    row_count = block_input.shape[2]
    model_width = block_input.shape[3]
    inner_local = in_weight.shape[3]
    inner_total = inner_local * part_count
    gain_norm = norm_gain[0]
    gain_gate = gate_gain[0]
    own_weight = jnp.concatenate([in_weight[0, :, 0], in_weight[0, :, 1], step_weight[0]], axis=1)
    shared_weight = state_weight[0]
    weight_out = out_weight[0]
    positions = part_index * row_count + jnp.arange(row_count, dtype=jnp.int32)
    live_masks = (positions[None, :] < lengths).astype(jnp.float32)
    first_inputs = block_input[:, 0]
    outer_grads = out_grad[:, 0]

    def front(rows_in):
        values = rows_in.astype(jnp.float32)
        row_scale = lax.rsqrt(jnp.mean(values * values, axis=1, keepdims=True) + epsilon)
        normal = (values * row_scale * gain_norm).astype(jnp.bfloat16)
        gathered = lax.all_gather(normal, "mp", axis=0, tiled=True)
        own_pre = jnp.dot(gathered, own_weight, preferred_element_type=jnp.float32)
        state_pre = jnp.dot(gathered, shared_weight, preferred_element_type=jnp.float32)
        gate_pre = own_pre[:, :inner_local]
        inner_pre = own_pre[:, inner_local : 2 * inner_local]
        step_pre = own_pre[:, 2 * inner_local :]
        (inner_act, state_act), conv_pull = jax.vjp(
            conv_front, inner_pre, state_pre, conv_inner[0], conv_state[0]
        )
        gated_out, core_pull = jax.vjp(
            mixer_core,
            gate_pre,
            round_trip(inner_act),
            round_trip(state_act),
            step_pre,
            step_bias[0],
            decay_log[0],
            skip_gain[0],
        )
        squares = lax.psum(jnp.sum(gated_out * gated_out, axis=1), "mp")
        inv_rms = lax.rsqrt(squares / inner_total + epsilon)[:, None]
        normed = (gated_out * inv_rms * gain_gate).astype(jnp.bfloat16)
        return (values, row_scale, gathered, conv_pull, core_pull, gated_out, inv_rms, normed)

    def project_out(normed):
        return lax.psum_scatter(
            jnp.dot(normed, weight_out, preferred_element_type=jnp.float32),
            "mp",
            scatter_dimension=0,
            tiled=True,
        )

    def input_back(own_grad):
        return lax.psum_scatter(
            jnp.einsum("lc,dc->ld", own_grad, own_weight, preferred_element_type=jnp.float32),
            "mp",
            scatter_dimension=0,
            tiled=True,
        )

    def forward_tick(tick_index, state_carry):
        incoming, outputs, inputs = state_carry
        position = tick_index - section_id
        is_live = (position >= 0) & (position < micro_count)
        slot_index = jnp.clip(position, 0, micro_count - 1)
        fresh = lax.dynamic_index_in_dim(first_inputs, slot_index, 0, keepdims=False)
        rows_in = jnp.where(section_id == 0, fresh, incoming)
        pieces = front(rows_in)
        branch = project_out(pieces[7])
        mask_col = lax.dynamic_index_in_dim(live_masks, slot_index, 0, keepdims=False)[:, None]
        result = (pieces[0] + mask_col * branch).astype(jnp.bfloat16)
        passed = shifted(result, "section", 1)
        outputs = jnp.where(
            is_live, lax.dynamic_update_index_in_dim(outputs, result, slot_index, 0), outputs
        )
        inputs = jnp.where(
            is_live, lax.dynamic_update_index_in_dim(inputs, rows_in, slot_index, 0), inputs
        )
        return (passed, outputs, inputs)

    forward_start = (
        jnp.zeros((row_count, model_width), jnp.bfloat16),
        jnp.zeros_like(first_inputs),
        jnp.zeros_like(first_inputs),
    )
    leftover, outputs, inputs = lax.fori_loop(0, micro_count + 1, forward_tick, forward_start)

    def backward_tick(tick_index, state_carry):
        incoming, in_grads, totals = state_carry
        position = tick_index - (1 - section_id)
        is_live = (position >= 0) & (position < micro_count)
        slot_index = jnp.clip(position, 0, micro_count - 1)
        rows_in = lax.dynamic_index_in_dim(inputs, slot_index, 0, keepdims=False)
        fresh_grad = lax.dynamic_index_in_dim(outer_grads, slot_index, 0, keepdims=False)
        grad_rows = jnp.where(section_id == 1, fresh_grad, incoming).astype(jnp.float32)
        values, row_scale, gathered, conv_pull, core_pull, gated_out, inv_rms, normed = front(
            rows_in
        )
        mask_col = lax.dynamic_index_in_dim(live_masks, slot_index, 0, keepdims=False)[:, None]
        branch_grad = (mask_col * grad_rows).astype(jnp.bfloat16)
        full_grad = lax.all_gather(branch_grad, "mp", axis=0, tiled=True)
        normed_grad = jnp.einsum(
            "ld,id->li", full_grad, weight_out, preferred_element_type=jnp.float32
        )
        out_part = jnp.einsum("li,ld->id", normed, full_grad, preferred_element_type=jnp.float32)
        gate_part = jnp.sum(normed_grad * gated_out * inv_rms, axis=0)
        scaled = normed_grad * gain_gate
        cross_sum = lax.psum(jnp.sum(scaled * gated_out, axis=1), "mp")[:, None]
        gated_grad = inv_rms * scaled - gated_out * inv_rms**3 * cross_sum / inner_total
        core_grads = core_pull(gated_grad)
        conv_grads = conv_pull((core_grads[1], core_grads[2]))
        state_grad = lax.psum(conv_grads[1], "mp").astype(jnp.bfloat16)
        own_grad = jnp.concatenate([core_grads[0], conv_grads[0], core_grads[3]], axis=1).astype(
            jnp.bfloat16
        )
        own_part = jnp.einsum("ld,lc->dc", gathered, own_grad, preferred_element_type=jnp.float32)
        shared_part = jnp.einsum(
            "ld,lc->dc", gathered, state_grad, preferred_element_type=jnp.float32
        )
        normal_grad = input_back(own_grad)
        own_state = lax.dynamic_slice_in_dim(state_grad, part_index * row_count, row_count, 0)
        normal_grad = normal_grad + jnp.einsum(
            "lc,dc->ld", own_state, shared_weight, preferred_element_type=jnp.float32
        )
        norm_part = jnp.sum(normal_grad * values * row_scale, axis=0)
        scaled_in = normal_grad * gain_norm
        input_grad = (
            grad_rows
            + row_scale * scaled_in
            - values * row_scale**3 * jnp.mean(scaled_in * values, axis=1, keepdims=True)
        )
        passed = shifted(input_grad.astype(jnp.bfloat16), "section", -1)
        in_grads = jnp.where(
            is_live, lax.dynamic_update_index_in_dim(in_grads, input_grad, slot_index, 0), in_grads
        )
        weight_live = is_live.astype(jnp.float32)
        fresh_parts = (
            own_part,
            shared_part,
            out_part,
            conv_grads[2],
            core_grads[4],
            core_grads[5],
            core_grads[6],
            gate_part,
            norm_part,
            conv_grads[3],
        )
        totals = tuple((summed + weight_live * piece for summed, piece in zip(totals, fresh_parts)))
        return (passed, in_grads, totals)

    zero_totals = (
        jnp.zeros(own_weight.shape, jnp.float32),
        jnp.zeros(shared_weight.shape, jnp.float32),
        jnp.zeros(weight_out.shape, jnp.float32),
        jnp.zeros(conv_inner[0].shape, jnp.float32),
        jnp.zeros(step_bias[0].shape, jnp.float32),
        jnp.zeros(decay_log[0].shape, jnp.float32),
        jnp.zeros(skip_gain[0].shape, jnp.float32),
        jnp.zeros(gain_gate.shape, jnp.float32),
        jnp.zeros(gain_norm.shape, jnp.float32),
        jnp.zeros(conv_state[0].shape, jnp.float32),
    )
    backward_start = (
        jnp.zeros((row_count, model_width), jnp.bfloat16),
        jnp.zeros(first_inputs.shape, jnp.float32),
        zero_totals,
    )
    leftover, in_grads, totals = lax.fori_loop(0, micro_count + 1, backward_tick, backward_start)
    reduced = lax.psum(
        (totals[0], totals[1], totals[2], totals[3], totals[4], totals[5], totals[6], totals[7]),
        "dp",
    )
    common = lax.psum((totals[8], totals[9]), ("dp", "mp"))
    own_total = reduced[0]
    grad_in_weight = jnp.stack(
        [own_total[:, :inner_local], own_total[:, inner_local : 2 * inner_local]], axis=1
    )[None]
    grad_step_weight = own_total[:, 2 * inner_local :][None]
    return (
        outputs[None, :, None],
        in_grads[None, :, None],
        common[0][None],
        grad_in_weight,
        reduced[1][None],
        grad_step_weight,
        reduced[3][None],
        common[1][None],
        reduced[4][None],
        reduced[5][None],
        reduced[6][None],
        reduced[7][None],
        reduced[2][None],
    )


def solution(mesh):
    return jax.shard_map(
        on_device,
        mesh=mesh,
        in_specs=(
            P(None, "dp", "mp", None),
            P(None, "dp", "mp", None),
            P(None, "dp"),
            P("section", None),
            P("section", None, None, "mp"),
            P("section", None, None),
            P("section", None, "mp"),
            P("section", None, "mp"),
            P("section", None, None),
            P("section", "mp"),
            P("section", "mp"),
            P("section", "mp"),
            P("section", "mp"),
            P("section", "mp", None),
        ),
        out_specs=(
            P("section", None, "dp", "mp", None),
            P("section", None, "dp", "mp", None),
            P("section", None),
            P("section", None, None, "mp"),
            P("section", None, None),
            P("section", None, "mp"),
            P("section", None, "mp"),
            P("section", None, None),
            P("section", "mp"),
            P("section", "mp"),
            P("section", "mp"),
            P("section", "mp"),
            P("section", "mp", None),
        ),
        check_vma=False,
    )
```

profile of v0, /device:TPU:0, one launch (start us, length us, event | category | flops | bytes accessed | tf_op | source)
XLA Modules:
  0.0 3261.7 jit_solution(17978206233384575531)
XLA Ops:
  8.2 17.8 fusion.188
  50.3 1090.5 %while.57 = (s32[]{:T(128)}, bf16[256,2048]{1,0:T(8,128)(2,1)}, bf16[2,256,2048]{2,1,0:T(8,128)(2,1)}, bf16[2,256,2048]{2,1,0:T(8,128)(2,1)S(1)}, pred[]{:T(512)...) while((s32[]{:T(128)}, bf16[256,2048]{1,0:T(8,128)(2,1)}, ...), condition=%wide.region_7.8_spmd, body=%wide.region_0.7_spmd.sunk | while | flops 20607027200 | bytes 256984368 | solution.py:192
  77.3 81.3 %all-gather.4.cloned.1.call-done = bf16[1024,2048]{1,0:T(8,128)(2,1)} async-done(((bf16[256,2048]{1,0:T(8,128)(2,1)}), bf16[1024,2048]{1,0:T(8,128)(2,1)}) %all-gather.4.cloned.1.call-update) | async-done | bytes 4194320 | tf_op jit(solution)/shard_map/while/body/eval_jaxpr/all_gather | solution.py:127
  158.6 15.0 fusion.345
  254.6 143.1 %reduce-scatter.3.cloned.1.call-done = f32[256,2048]{1,0:T(8,128)} async-done(((f32[1024,2048]{1,0:T(8,128)}), f32[256,2048]{1,0:T(8,128)}) %reduce-scatter.3.cloned.1.call-update) | async-done | bytes 2097168 | tf_op jit(solution)/shard_map/while/body/eval_jaxpr/reduce_scatter | solution.py:152
  405.0 22.2 collective-permute-done
  434.4 80.4 %all-gather.4.cloned.1.call-done = bf16[1024,2048]{1,0:T(8,128)(2,1)} async-done(((bf16[256,2048]{1,0:T(8,128)(2,1)}), bf16[1024,2048]{1,0:T(8,128)(2,1)}) %all-gather.4.cloned.1.call-update) | async-done | bytes 4194320 | tf_op jit(solution)/shard_map/while/body/eval_jaxpr/all_gather | solution.py:127
  514.8 15.0 fusion.345
  610.8 143.1 %reduce-scatter.3.cloned.1.call-done = f32[256,2048]{1,0:T(8,128)} async-done(((f32[1024,2048]{1,0:T(8,128)}), f32[256,2048]{1,0:T(8,128)}) %reduce-scatter.3.cloned.1.call-update) | async-done | bytes 2097168 | tf_op jit(solution)/shard_map/while/body/eval_jaxpr/reduce_scatter | solution.py:152
  761.3 22.2 collective-permute-done
  790.7 80.4 %all-gather.4.cloned.1.call-done = bf16[1024,2048]{1,0:T(8,128)(2,1)} async-done(((bf16[256,2048]{1,0:T(8,128)(2,1)}), bf16[1024,2048]{1,0:T(8,128)(2,1)}) %all-gather.4.cloned.1.call-update) | async-done | bytes 4194320 | tf_op jit(solution)/shard_map/while/body/eval_jaxpr/all_gather | solution.py:127
  871.1 15.0 fusion.345
  967.1 143.1 %reduce-scatter.3.cloned.1.call-done = f32[256,2048]{1,0:T(8,128)} async-done(((f32[1024,2048]{1,0:T(8,128)}), f32[256,2048]{1,0:T(8,128)}) %reduce-scatter.3.cloned.1.call-update) | async-done | bytes 2097168 | tf_op jit(solution)/shard_map/while/body/eval_jaxpr/reduce_scatter | solution.py:152
  1117.5 22.3 collective-permute-done
  1143.4 1564.9 %while.58 = (s32[]{:T(128)}, bf16[256,2048]{1,0:T(8,128)(2,1)S(1)}, f32[2,256,2048]{2,1,0:T(8,128)}, f32[2048,2064]{0,1:T(8,128)}, f32[2048,256]{1,0:T(8,128)}, ...) while((s32[]{:T(128)}, bf16[256,2048]{1,0:T(8,128)(2,1)S(1)}, ...), condition=%wide.region_45.46_spmd.clone, body=%wide.region_8.45_spmd.clone.sunk | while | flops 57461940224 | bytes 846677184 | solution.py:275
  1157.9 78.2 %all-gather.6.cloned.1.call-done = bf16[1024,2048]{1,0:T(8,128)(2,1)} async-done(((bf16[256,2048]{1,0:T(8,128)(2,1)}), bf16[1024,2048]{1,0:T(8,128)(2,1)}) %all-gather.6.cloned.1.call-update) | async-done | bytes 4194320 | tf_op jit(solution)/shard_map/while/body/eval_jaxpr/all_gather | solution.py:127
  1236.1 15.0 fusion.392
  1284.9 14.1 fusion.403
  1356.7 22.2 fusion.405
  1387.8 15.8 bitcast_add_fusion.8
  1443.4 16.0 fusion.414
  1480.4 73.9 %all-reduce.36 = bf16[1024,256]{1,0:T(8,128)(2,1)} all-reduce(f32[1024,256]{1,0:T(8,128)S(1)} %pad_add_fusion.10), channel_id=1, replica_groups=mesh['section'=2,'dp'=4,'mp'=4] {'mp'}, use_global_device_ids=true, to_apply=%region_29.29 | all-reduce | flops 262144 | bytes 1572864 | tf_op jit(solution)/shard_map/while/body/eval_jaxpr/psum | solution.py:218
  1565.8 15.9 select_add_fusion.12
  1581.7 54.1 %reduce-scatter.5.cloned.1.call-done = f32[256,2048]{1,0:T(8,128)} async-done(((f32[1024,2048]{1,0:T(8,128)}), f32[256,2048]{1,0:T(8,128)}) %reduce-scatter.5.cloned.1.call-update) | async-done | bytes 2097168 | tf_op jit(solution)/shard_map/while/body/eval_jaxpr/reduce_scatter | solution.py:160
  1646.7 22.5 collective-permute-done.1
  1677.0 76.1 %all-gather.6.cloned.1.call-done = bf16[1024,2048]{1,0:T(8,128)(2,1)} async-done(((bf16[256,2048]{1,0:T(8,128)(2,1)}), bf16[1024,2048]{1,0:T(8,128)(2,1)}) %all-gather.6.cloned.1.call-update) | async-done | bytes 4194320 | tf_op jit(solution)/shard_map/while/body/eval_jaxpr/all_gather | solution.py:127
  1753.0 15.0 fusion.392
  1873.7 22.4 fusion.405
  1905.0 15.6 bitcast_add_fusion.8
  1960.3 16.2 fusion.414
  1997.3 73.9 %all-reduce.36 = bf16[1024,256]{1,0:T(8,128)(2,1)} all-reduce(f32[1024,256]{1,0:T(8,128)S(1)} %pad_add_fusion.10), channel_id=1, replica_groups=mesh['section'=2,'dp'=4,'mp'=4] {'mp'}, use_global_device_ids=true, to_apply=%region_29.29 | all-reduce | flops 262144 | bytes 1572864 | tf_op jit(solution)/shard_map/while/body/eval_jaxpr/psum | solution.py:218
  2085.2 18.3 select_add_fusion.12
  2103.6 49.4 %reduce-scatter.5.cloned.1.call-done = f32[256,2048]{1,0:T(8,128)} async-done(((f32[1024,2048]{1,0:T(8,128)}), f32[256,2048]{1,0:T(8,128)}) %reduce-scatter.5.cloned.1.call-update) | async-done | bytes 2097168 | tf_op jit(solution)/shard_map/while/body/eval_jaxpr/reduce_scatter | solution.py:160
  2163.9 22.5 collective-permute-done.1
  2194.3 76.4 %all-gather.6.cloned.1.call-done = bf16[1024,2048]{1,0:T(8,128)(2,1)} async-done(((bf16[256,2048]{1,0:T(8,128)(2,1)}), bf16[1024,2048]{1,0:T(8,128)(2,1)}) %all-gather.6.cloned.1.call-update) | async-done | bytes 4194320 | tf_op jit(solution)/shard_map/while/body/eval_jaxpr/all_gather | solution.py:127
  2270.7 15.0 fusion.392
  2391.3 22.2 fusion.405
  2422.4 15.6 bitcast_add_fusion.8
  2477.8 16.2 fusion.414
  2514.9 73.9 %all-reduce.36 = bf16[1024,256]{1,0:T(8,128)(2,1)} all-reduce(f32[1024,256]{1,0:T(8,128)S(1)} %pad_add_fusion.10), channel_id=1, replica_groups=mesh['section'=2,'dp'=4,'mp'=4] {'mp'}, use_global_device_ids=true, to_apply=%region_29.29 | all-reduce | flops 262144 | bytes 1572864 | tf_op jit(solution)/shard_map/while/body/eval_jaxpr/psum | solution.py:218
  2588.8 14.0 select_add_fusion.13
  2602.8 18.3 select_add_fusion.12
  2621.1 49.4 %reduce-scatter.5.cloned.1.call-done = f32[256,2048]{1,0:T(8,128)} async-done(((f32[1024,2048]{1,0:T(8,128)}), f32[256,2048]{1,0:T(8,128)}) %reduce-scatter.5.cloned.1.call-update) | async-done | bytes 2097168 | tf_op jit(solution)/shard_map/while/body/eval_jaxpr/reduce_scatter | solution.py:160
  2681.5 22.5 collective-permute-done.1
  2708.4 17.0 copy.251
  2726.1 62.1 %all-reduce.29 = (f32[1,2048]{1,0:T(1,128)}, f32[1,4,256]{2,1,0:T(4,128)}) all-reduce(f32[1,2048]{1,0:T(1,128)S(1)} %bitcast.799, f32[1,4,256]{2,1,0:T(4,128)S(1)} %bitcast.809), channel_id=1, replica_groups=mesh['section'=2,'dp'=4,'mp'=4] {'dp','mp'}, use_global_device_ids=true, to_apply=%region_46.47 | all-reduce | flops 3072 | bytes 24576 | tf_op jit(solution)/shard_map/psum | solution.py:280
  2801.1 399.1 %all-reduce.35.cloned.1.call-done = (f32[2048,2064]{1,0:T(8,128)}, f32[1,2048,256]{2,1,0:T(8,128)}, f32[1,1024,2048]{2,1,0:T(8,128)}) async-done(((f32[2048,2064]{1,0:T(8,128)}, f32[1,2048,256]{2,1,0:T(8,128)}, f32[1,1024,2048]{2,1,0:T(8,128)}), (f32[2048,2064]{1,0:T(8,128)}, f32[1,2048,256]{2,1,0:T(8,128)}, f32[1,1024,2048]{2,1,0:T(8,128)})) %all-reduce.35.cloned.1.call-update) | async-done | bytes 27394064 | tf_op jit(solution)/shard_map/psum | solution.py:276
  3219.1 25.1 copy.252
  (1167 shorter events, 943.1 us)
Async XLA Ops:
  71.1 107.8 %copy-start.89 = (f32[1,1,16]{2,1,0:T(1,128)}, f32[1,1,16]{2,1,0:T(1,128)S(1)}, u32[]{:S(2)}) copy-start(f32[1,1,16]{2,1,0:T(1,128)S(1)} %get-tuple-element.1962) | copy-start | bytes 196 | tf_op jit(solution)/shard_map/while
  71.1 87.5 %all-gather.4.cloned.1.call-start = ((), (), s32[]{:S(2)}) async-start(), calls=%async_computation.3 | async-start | bytes 5242880 | tf_op jit(solution)/shard_map/while/body/eval_jaxpr/all_gather | solution.py:127
  74.7 323.0 %reduce-scatter.3.cloned.1.call-start = ((), (), s32[]{:S(2)}) async-start(), calls=%async_computation.4 | async-start | bytes 10485760 | tf_op jit(solution)/shard_map/while/body/eval_jaxpr/reduce_scatter | solution.py:152
  253.9 174.4 %copy-start.48 = (f32[1,4,1024]{2,1,0:T(4,128)S(1)}, f32[1,4,1024]{2,1,0:T(4,128)}, u32[]{:S(2)}) copy-start(f32[1,4,1024]{2,1,0:T(4,128)} %get-tuple-element.2151) | copy-start | bytes 49156 | tf_op jit(solution)/shard_map/while
  253.9 174.4 %copy-start.90 = (f32[1,1,16]{2,1,0:T(1,128)S(1)}, f32[1,1,16]{2,1,0:T(1,128)}, u32[]{:S(2)}) copy-start(f32[1,1,16]{2,1,0:T(1,128)} %copy-done.89) | copy-start | bytes 196 | tf_op jit(solution)/shard_map/while
  401.6 25.7 collective-permute-start
  428.2 106.9 %copy-start.89 = (f32[1,1,16]{2,1,0:T(1,128)}, f32[1,1,16]{2,1,0:T(1,128)S(1)}, u32[]{:S(2)}) copy-start(f32[1,1,16]{2,1,0:T(1,128)S(1)} %get-tuple-element.1962) | copy-start | bytes 196 | tf_op jit(solution)/shard_map/while
  428.3 86.6 %all-gather.4.cloned.1.call-start = ((), (), s32[]{:S(2)}) async-start(), calls=%async_computation.3 | async-start | bytes 5242880 | tf_op jit(solution)/shard_map/while/body/eval_jaxpr/all_gather | solution.py:127
  431.8 322.1 %reduce-scatter.3.cloned.1.call-start = ((), (), s32[]{:S(2)}) async-start(), calls=%async_computation.4 | async-start | bytes 10485760 | tf_op jit(solution)/shard_map/while/body/eval_jaxpr/reduce_scatter | solution.py:152
  610.1 174.4 %copy-start.48 = (f32[1,4,1024]{2,1,0:T(4,128)S(1)}, f32[1,4,1024]{2,1,0:T(4,128)}, u32[]{:S(2)}) copy-start(f32[1,4,1024]{2,1,0:T(4,128)} %get-tuple-element.2151) | copy-start | bytes 49156 | tf_op jit(solution)/shard_map/while
  610.1 174.4 %copy-start.90 = (f32[1,1,16]{2,1,0:T(1,128)S(1)}, f32[1,1,16]{2,1,0:T(1,128)}, u32[]{:S(2)}) copy-start(f32[1,1,16]{2,1,0:T(1,128)} %copy-done.89) | copy-start | bytes 196 | tf_op jit(solution)/shard_map/while
  757.8 25.7 collective-permute-start
  784.5 86.6 %all-gather.4.cloned.1.call-start = ((), (), s32[]{:S(2)}) async-start(), calls=%async_computation.3 | async-start | bytes 5242880 | tf_op jit(solution)/shard_map/while/body/eval_jaxpr/all_gather | solution.py:127
  788.0 322.1 %reduce-scatter.3.cloned.1.call-start = ((), (), s32[]{:S(2)}) async-start(), calls=%async_computation.4 | async-start | bytes 10485760 | tf_op jit(solution)/shard_map/while/body/eval_jaxpr/reduce_scatter | solution.py:152
  966.4 174.4 %copy-start.48 = (f32[1,4,1024]{2,1,0:T(4,128)S(1)}, f32[1,4,1024]{2,1,0:T(4,128)}, u32[]{:S(2)}) copy-start(f32[1,4,1024]{2,1,0:T(4,128)} %get-tuple-element.2151) | copy-start | bytes 49156 | tf_op jit(solution)/shard_map/while
  966.4 174.4 %copy-start.90 = (f32[1,1,16]{2,1,0:T(1,128)S(1)}, f32[1,1,16]{2,1,0:T(1,128)}, u32[]{:S(2)}) copy-start(f32[1,1,16]{2,1,0:T(1,128)} %copy-done.89) | copy-start | bytes 196 | tf_op jit(solution)/shard_map/while
  1114.1 25.7 collective-permute-start
  1150.5 117.5 %copy-start.91 = (f32[1,1,16]{2,1,0:T(1,128)}, f32[1,1,16]{2,1,0:T(1,128)S(1)}, u32[]{:S(2)}) copy-start(f32[1,1,16]{2,1,0:T(1,128)S(1)} %get-tuple-element.2064) | copy-start | bytes 196 | tf_op jit(solution)/shard_map/while
  1150.5 85.6 %all-gather.6.cloned.1.call-start = ((), (), s32[]{:S(2)}) async-start(), calls=%async_computation.5 | async-start | bytes 5242880 | tf_op jit(solution)/shard_map/while/body/eval_jaxpr/all_gather | solution.py:127
  1153.1 166.0 %all-gather.8.cloned.1.call-start = ((), (), s32[]{:S(2)}) async-start(), calls=%async_computation.6 | async-start | bytes 5242880 | tf_op jit(solution)/shard_map/while/body/eval_jaxpr/all_gather | solution.py:207
  1156.4 479.4 %reduce-scatter.5.cloned.1.call-start = ((), (), s32[]{:S(2)}) async-start(), calls=%async_computation.7 | async-start | bytes 10485760 | tf_op jit(solution)/shard_map/while/body/eval_jaxpr/reduce_scatter | solution.py:160
  1156.5 126.4 %copy-start.41 = (pred[256,256]{1,0:T(8,128)(4,1)}, pred[256,256]{1,0:T(8,128)(4,1)S(1)}, u32[]{:S(2)}) copy-start(pred[256,256]{1,0:T(8,128)(4,1)S(1)} %iota_compare_fusion.5) | copy-start | bytes 196612 | tf_op jit(solution)/shard_map/while
  1157.4 116.9 %copy-start.69 = (f32[1,1,256]{2,1,0:T(1,128)}, f32[1,1,256]{2,1,0:T(1,128)S(1)}, u32[]{:S(2)}) copy-start(f32[1,1,256]{2,1,0:T(1,128)S(1)} %get-tuple-element.1830) | copy-start | bytes 3076 | tf_op jit(solution)/shard_map/while
  1157.4 116.9 %copy-start.71 = (f32[1,1,256]{2,1,0:T(1,128)}, f32[1,1,256]{2,1,0:T(1,128)S(1)}, u32[]{:S(2)}) copy-start(f32[1,1,256]{2,1,0:T(1,128)S(1)} %get-tuple-element.1827) | copy-start | bytes 3076 | tf_op jit(solution)/shard_map/while
  1157.4 116.9 %copy-start.73 = (f32[1,1,256]{2,1,0:T(1,128)}, f32[1,1,256]{2,1,0:T(1,128)S(1)}, u32[]{:S(2)}) copy-start(f32[1,1,256]{2,1,0:T(1,128)S(1)} %get-tuple-element.1828) | copy-start | bytes 3076 | tf_op jit(solution)/shard_map/while
  1157.4 116.9 %copy-start.75 = (f32[1,1,256]{2,1,0:T(1,128)}, f32[1,1,256]{2,1,0:T(1,128)S(1)}, u32[]{:S(2)}) copy-start(f32[1,1,256]{2,1,0:T(1,128)S(1)} %get-tuple-element.1829) | copy-start | bytes 3076 | tf_op jit(solution)/shard_map/while
  1642.9 26.4 collective-permute-start.1
  1669.5 115.4 %copy-start.91 = (f32[1,1,16]{2,1,0:T(1,128)}, f32[1,1,16]{2,1,0:T(1,128)S(1)}, u32[]{:S(2)}) copy-start(f32[1,1,16]{2,1,0:T(1,128)S(1)} %get-tuple-element.2064) | copy-start | bytes 196 | tf_op jit(solution)/shard_map/while
  1669.5 83.5 %all-gather.6.cloned.1.call-start = ((), (), s32[]{:S(2)}) async-start(), calls=%async_computation.5 | async-start | bytes 5242880 | tf_op jit(solution)/shard_map/while/body/eval_jaxpr/all_gather | solution.py:127
  1672.1 163.9 %all-gather.8.cloned.1.call-start = ((), (), s32[]{:S(2)}) async-start(), calls=%async_computation.6 | async-start | bytes 5242880 | tf_op jit(solution)/shard_map/while/body/eval_jaxpr/all_gather | solution.py:207
  1675.4 477.5 %reduce-scatter.5.cloned.1.call-start = ((), (), s32[]{:S(2)}) async-start(), calls=%async_computation.7 | async-start | bytes 10485760 | tf_op jit(solution)/shard_map/while/body/eval_jaxpr/reduce_scatter | solution.py:160
  1675.5 124.5 %copy-start.41 = (pred[256,256]{1,0:T(8,128)(4,1)}, pred[256,256]{1,0:T(8,128)(4,1)S(1)}, u32[]{:S(2)}) copy-start(pred[256,256]{1,0:T(8,128)(4,1)S(1)} %iota_compare_fusion.5) | copy-start | bytes 196612 | tf_op jit(solution)/shard_map/while
  1676.4 115.0 %copy-start.69 = (f32[1,1,256]{2,1,0:T(1,128)}, f32[1,1,256]{2,1,0:T(1,128)S(1)}, u32[]{:S(2)}) copy-start(f32[1,1,256]{2,1,0:T(1,128)S(1)} %get-tuple-element.1830) | copy-start | bytes 3076 | tf_op jit(solution)/shard_map/while
  1676.4 115.0 %copy-start.71 = (f32[1,1,256]{2,1,0:T(1,128)}, f32[1,1,256]{2,1,0:T(1,128)S(1)}, u32[]{:S(2)}) copy-start(f32[1,1,256]{2,1,0:T(1,128)S(1)} %get-tuple-element.1827) | copy-start | bytes 3076 | tf_op jit(solution)/shard_map/while
  1676.4 115.0 %copy-start.73 = (f32[1,1,256]{2,1,0:T(1,128)}, f32[1,1,256]{2,1,0:T(1,128)S(1)}, u32[]{:S(2)}) copy-start(f32[1,1,256]{2,1,0:T(1,128)S(1)} %get-tuple-element.1828) | copy-start | bytes 3076 | tf_op jit(solution)/shard_map/while
  1676.4 115.0 %copy-start.75 = (f32[1,1,256]{2,1,0:T(1,128)}, f32[1,1,256]{2,1,0:T(1,128)S(1)}, u32[]{:S(2)}) copy-start(f32[1,1,256]{2,1,0:T(1,128)S(1)} %get-tuple-element.1829) | copy-start | bytes 3076 | tf_op jit(solution)/shard_map/while
  2160.0 26.4 collective-permute-start.1
  2186.9 115.7 %copy-start.91 = (f32[1,1,16]{2,1,0:T(1,128)}, f32[1,1,16]{2,1,0:T(1,128)S(1)}, u32[]{:S(2)}) copy-start(f32[1,1,16]{2,1,0:T(1,128)S(1)} %get-tuple-element.2064) | copy-start | bytes 196 | tf_op jit(solution)/shard_map/while
  2186.9 83.8 %all-gather.6.cloned.1.call-start = ((), (), s32[]{:S(2)}) async-start(), calls=%async_computation.5 | async-start | bytes 5242880 | tf_op jit(solution)/shard_map/while/body/eval_jaxpr/all_gather | solution.py:127
  2189.5 164.2 %all-gather.8.cloned.1.call-start = ((), (), s32[]{:S(2)}) async-start(), calls=%async_computation.6 | async-start | bytes 5242880 | tf_op jit(solution)/shard_map/while/body/eval_jaxpr/all_gather | solution.py:207
  2192.8 477.7 %reduce-scatter.5.cloned.1.call-start = ((), (), s32[]{:S(2)}) async-start(), calls=%async_computation.7 | async-start | bytes 10485760 | tf_op jit(solution)/shard_map/while/body/eval_jaxpr/reduce_scatter | solution.py:160
  2192.9 124.5 %copy-start.41 = (pred[256,256]{1,0:T(8,128)(4,1)}, pred[256,256]{1,0:T(8,128)(4,1)S(1)}, u32[]{:S(2)}) copy-start(pred[256,256]{1,0:T(8,128)(4,1)S(1)} %iota_compare_fusion.5) | copy-start | bytes 196612 | tf_op jit(solution)/shard_map/while
  2193.8 115.0 %copy-start.69 = (f32[1,1,256]{2,1,0:T(1,128)}, f32[1,1,256]{2,1,0:T(1,128)S(1)}, u32[]{:S(2)}) copy-start(f32[1,1,256]{2,1,0:T(1,128)S(1)} %get-tuple-element.1830) | copy-start | bytes 3076 | tf_op jit(solution)/shard_map/while
  2193.8 115.0 %copy-start.71 = (f32[1,1,256]{2,1,0:T(1,128)}, f32[1,1,256]{2,1,0:T(1,128)S(1)}, u32[]{:S(2)}) copy-start(f32[1,1,256]{2,1,0:T(1,128)S(1)} %get-tuple-element.1827) | copy-start | bytes 3076 | tf_op jit(solution)/shard_map/while
  2193.8 115.0 %copy-start.73 = (f32[1,1,256]{2,1,0:T(1,128)}, f32[1,1,256]{2,1,0:T(1,128)S(1)}, u32[]{:S(2)}) copy-start(f32[1,1,256]{2,1,0:T(1,128)S(1)} %get-tuple-element.1828) | copy-start | bytes 3076 | tf_op jit(solution)/shard_map/while
  2193.8 115.0 %copy-start.75 = (f32[1,1,256]{2,1,0:T(1,128)}, f32[1,1,256]{2,1,0:T(1,128)S(1)}, u32[]{:S(2)}) copy-start(f32[1,1,256]{2,1,0:T(1,128)S(1)} %get-tuple-element.1829) | copy-start | bytes 3076 | tf_op jit(solution)/shard_map/while
  2677.6 26.4 collective-permute-start.1
  2708.3 491.9 %all-reduce.35.cloned.1.call-start = ((), (), s32[]{:S(2)}) async-start(), calls=%async_computation.2 | async-start | bytes 56623104 | tf_op jit(solution)/shard_map/psum | solution.py:276
  (329 other events, 5117.3 us)
Sparse Core Ops, SparseCore 0:
  74.8 83.7 all-gather.3
  254.0 143.6 reduce-scatter.2
  431.9 82.8 all-gather.3
  610.2 143.6 reduce-scatter.2
  788.2 82.8 all-gather.3
  966.5 143.6 reduce-scatter.2
  1153.5 82.5 all-gather.5
  1237.7 79.4 all-gather.7
  1459.5 176.2 reduce-scatter.4
  1672.2 80.7 all-gather.5
  1754.6 79.4 all-gather.7
  1976.6 176.2 reduce-scatter.4
  2189.9 80.7 all-gather.5
  2272.1 79.4 all-gather.7
  2494.2 176.2 reduce-scatter.4
Sparse Core Ops, SparseCore 1:
  2725.6 474.6 all-reduce.34
where the time goes:
time: 3270 us; the launch traced here: 3260 us
  waiting for transfers between devices  1590 us (49%)
  matrix products  637 us (19%)
  blocking collectives  381 us (12%)
  other arithmetic  322 us (10%)
  local copies, waits for them, and re-layouts  264 us (8%)
  loops' own time  38.6 us (1%)
    all_gather x6, waiting for transfers between devices, front(): gathered = lax.all_gather(normal, 'mp', axis=0, tiled=True)  473 us
    reduce_scatter x3, waiting for transfers between devices, project_out(): lax.psum_scatter(jnp.dot(normed, weight_out, preferred_element_type=jnp.f...  429 us
    psum x1, waiting for transfers between devices, on_device(): lax.psum((totals[0], totals[1], totals[2], totals[3], totals[4], totals[5...  399 us
    psum x3, blocking collectives, backward_tick(): state_grad = lax.psum(conv_grads[1], 'mp').astype(jnp.bfloat16)  222 us
    dot_general x12, matrix products, state_scan(): within = jnp.einsum('ktsh,kshp->kthp', weights, x_blocks, precision=highest)  196 us
    reduce_scatter x3, waiting for transfers between devices, input_back(): lax.psum_scatter(jnp.einsum('lc,dc->ld', own_grad, own_weight, preferred_...  153 us
    ppermute x6, waiting for transfers between devices, shifted(): return lax.ppermute(value, axis, pairs)  134 us
    dot_general x6, matrix products, front(): own_pre = jnp.dot(gathered, own_weight, preferred_element_type=jnp.float32)  89.9 us
  transfers between devices with their start and end apart: 22, of which 19 were waited for; matrix products, arithmetic and copies ran while one was open for 12% of the time, Pallas kernels for 0%

commit v1 on v0

v1 whole, which is shorter than its diff:
```python
import functools
import jax
import jax.numpy as jnp
from jax import lax
from jax.experimental import pallas as pl
from jax.experimental.pallas import tpu as pltpu
from jax.sharding import PartitionSpec as P

epsilon = 1e-05
f32 = jnp.float32
bf16 = jnp.bfloat16
highest = lax.Precision.HIGHEST
BLOCK = 256
HALO = 8
LOG2E = 1.4426950408889634


def mm(a, b, contract, precision=None):
    return lax.dot_general(a, b, (contract, ((), ())), preferred_element_type=f32, precision=precision)


NN = ((1,), (0,))
NT = ((1,), (1,))
TN = ((0,), (0,))


def sigmoid(v):
    return 0.5 * jnp.tanh(0.5 * v) + 0.5


def step_of(z):
    e = jnp.exp(-jnp.abs(z))
    u = 1.0 + e
    d = u - 1.0
    tail = jnp.where(d == 0.0, e, jnp.log(u) * (e / jnp.where(d == 0.0, 1.0, d)))
    return jnp.maximum(z, 0.0) + tail


def triangle(inclusive, upper=False):
    r = lax.broadcasted_iota(jnp.int32, (BLOCK, BLOCK), 0)
    c = lax.broadcasted_iota(jnp.int32, (BLOCK, BLOCK), 1)
    if upper:
        r, c = c, r
    return (r >= c) if inclusive else (r > c)


def pad_lanes(v, to=128):
    return jnp.concatenate([v, jnp.zeros((v.shape[0], to - v.shape[1]), v.dtype)], axis=1)


def low_half(shape):
    return lax.broadcasted_iota(jnp.int32, shape, 1) < 64


def pair_of(cols, p):
    rows = cols.shape[0]
    lo = low_half((rows, 128))
    return jnp.where(lo, cols[:, 2 * p : 2 * p + 1], cols[:, 2 * p + 1 : 2 * p + 2])


def block_setup(step_pre, bias, decay, heads):
    z = step_pre + bias
    step = step_of(z)
    rate = jnp.exp(decay)
    dec = pad_lanes(step * rate)
    tri = triangle(True).astype(f32)
    ld = -mm(tri, dec, NN, highest)[:, :heads]
    return z, step, rate, ld


def fwd_kernel(sizes, pre, taps, heads3, gain, mixed, scaled, sq, states, ext, carry, scr):
    inner, state, heads = sizes
    k = pl.program_id(0)
    nst = state // 2
    pairs = heads // 2
    a_state, a_step = 2 * inner, 2 * inner + state

    @pl.when(k == 0)
    def _():
        ext[0:HALO, :] = jnp.zeros((HALO, inner + state), f32)
        carry[...] = jnp.zeros_like(carry)

    ext[HALO:, :] = pre[:, inner:a_step]

    def act(lo, width):
        c = taps[0:1, lo : lo + width] * ext[HALO - 3 : HALO - 3 + BLOCK, lo : lo + width]
        for j in range(1, 4):
            c = c + taps[j : j + 1, lo : lo + width] * ext[HALO - 3 + j : HALO - 3 + j + BLOCK, lo : lo + width]
        return (c * sigmoid(c)).astype(bf16)

    b = act(inner, nst)
    c = act(inner + nst, nst)
    z, step, rate, ld = block_setup(pre[:, a_step : a_step + heads], heads3[0:1, :heads], heads3[1:2, :heads], heads)
    ld2 = ld * LOG2E
    rrow = jnp.transpose(pad_lanes(jnp.log2(step) - ld2))
    eld = jnp.exp2(ld2)
    last = ld2[BLOCK - 1 : BLOCK, :]
    tail = jnp.exp2(last - ld2) * step
    scr[...] = jnp.where(triangle(True), mm(c, b, NT), 0.0)
    squares = jnp.zeros((BLOCK, 1), f32)
    half = BLOCK // 2
    for p in range(pairs):
        lanes = slice(128 * p, 128 * p + 128)
        x = act(128 * p, 128)
        xf = x.astype(f32)
        lo = low_half((BLOCK, 128))
        xs = [jnp.where(lo, x, jnp.zeros_like(x)), jnp.where(lo, jnp.zeros_like(x), x)]
        tops, bottoms = [], []
        for i in range(2):
            h = 2 * p + i
            top = jnp.exp2(jnp.minimum(ld2[:half, h : h + 1] + rrow[h : h + 1, :half], 40.0)) * scr[:half, :half]
            tops.append(mm(top.astype(bf16), xs[i][:half], NN))
            bot = jnp.exp2(jnp.minimum(ld2[half:, h : h + 1] + rrow[h : h + 1, :], 40.0)) * scr[half:, :]
            bottoms.append(mm(bot.astype(bf16), xs[i], NN))
        within = jnp.concatenate([tops[0] + tops[1], bottoms[0] + bottoms[1]], axis=0)
        s_in = carry[:, lanes]
        e_pair = pair_of(eld, p)
        cross = mm(c, s_in.astype(bf16), NN) * e_pair
        y = within + cross + pair_of(heads3[2:3, :heads], p) * xf
        mixed[:, lanes] = y
        g = pre[:, lanes]
        gated = y * (g * sigmoid(g))
        squares = squares + jnp.sum(gated * gated, axis=1, keepdims=True)
        scaled[:, lanes] = (gated * gain[:, lanes]).astype(bf16)
        s_out = e_pair[BLOCK - 1 :, :] * s_in + mm(b, (xf * pair_of(tail, p)).astype(bf16), TN)
        carry[:, lanes] = s_out
        states[0, :, lanes] = s_out
    sq[...] = squares
    ext[0:HALO, :] = ext[BLOCK : BLOCK + HALO, :]


def mix_forward(pre, taps, heads3, gain, inner, state, heads):
    rows = pre.shape[0]
    blocks = rows // BLOCK
    width = pre.shape[1]
    nst = state // 2
    return pl.pallas_call(
        functools.partial(fwd_kernel, (inner, state, heads)),
        grid=(blocks,),
        in_specs=[
            pl.BlockSpec((BLOCK, width), lambda k: (k, 0)),
            pl.BlockSpec((4, inner + state), lambda k: (0, 0)),
            pl.BlockSpec((3, heads), lambda k: (0, 0)),
            pl.BlockSpec((1, inner), lambda k: (0, 0)),
        ],
        out_specs=[
            pl.BlockSpec((BLOCK, inner), lambda k: (k, 0)),
            pl.BlockSpec((BLOCK, inner), lambda k: (k, 0)),
            pl.BlockSpec((BLOCK, 1), lambda k: (k, 0)),
            pl.BlockSpec((1, nst, inner), lambda k: (k, 0, 0)),
        ],
        out_shape=[
            jax.ShapeDtypeStruct((rows, inner), f32),
            jax.ShapeDtypeStruct((rows, inner), bf16),
            jax.ShapeDtypeStruct((rows, 1), f32),
            jax.ShapeDtypeStruct((blocks, nst, inner), f32),
        ],
        scratch_shapes=[
            pltpu.VMEM((BLOCK + HALO, inner + state), f32),
            pltpu.VMEM((nst, inner), f32),
            pltpu.VMEM((BLOCK, BLOCK), f32),
        ],
        name="mix_forward",
    )(pre, taps, heads3, gain)


def bwd_kernel(sizes, pre, halo, mixed, ngrad, rows2, s_in_ref, taps, heads3, gain,
               own, normed, g_taps, g_heads, g_gain, ext, dext, carry, acc, scr, dyb, xb, cold, rowd, xw):
    inner, state, heads = sizes
    step_id = pl.program_id(0)
    blocks = pl.num_programs(0)
    k = blocks - 1 - step_id
    nst = state // 2
    pairs = heads // 2
    a_state, a_step = 2 * inner, 2 * inner + state

    @pl.when(step_id == 0)
    def _():
        dext[BLOCK:, :] = jnp.zeros((HALO, inner + state), f32)
        carry[...] = jnp.zeros_like(carry)
        g_taps[...] = jnp.zeros_like(g_taps)
        g_heads[...] = jnp.zeros_like(g_heads)
        g_gain[...] = jnp.zeros_like(g_gain)

    ext[HALO:, :] = pre[:, inner:a_step]
    ext[0:HALO, :] = jnp.where(k == 0, 0.0, halo[:, inner:a_step])

    def conv(lo, width):
        c = taps[0:1, lo : lo + width] * ext[HALO - 3 : HALO - 3 + BLOCK, lo : lo + width]
        for j in range(1, 4):
            c = c + taps[j : j + 1, lo : lo + width] * ext[HALO - 3 + j : HALO - 3 + j + BLOCK, lo : lo + width]
        return c

    def dsilu(v):
        s = sigmoid(v)
        return s * (1.0 + v * (1.0 - s))

    cb = conv(inner, nst)
    cc = conv(inner + nst, nst)
    b = (cb * sigmoid(cb)).astype(bf16)
    c = (cc * sigmoid(cc)).astype(bf16)
    z, step, rate, ld = block_setup(pre[:, a_step : a_step + heads], heads3[0:1, :heads], heads3[1:2, :heads], heads)
    ld2 = ld * LOG2E
    ldrow = jnp.transpose(pad_lanes(ld2))
    rcol = jnp.log2(step) - ld2
    eld = jnp.exp2(ld2)
    tail = jnp.exp2(ld2[BLOCK - 1 : BLOCK, :] - ld2) * step
    scr[...] = jnp.where(triangle(True, upper=True), mm(b, c, NT), 0.0)
    acc[...] = jnp.zeros_like(acc)
    half = BLOCK // 2
    inv = rows2[:, 0:1]
    pull = rows2[:, 1:2]
    d_b = jnp.zeros((BLOCK, nst), f32)
    d_c = jnp.zeros((BLOCK, nst), f32)
    head_lane = lax.broadcasted_iota(jnp.int32, (1, 128), 1)
    cold[...] = jnp.zeros_like(cold)
    xw[...] = jnp.zeros_like(xw)
    carried = jnp.zeros((1, 128), f32)
    skips = jnp.zeros((1, 128), f32)
    for p in range(pairs):
        lanes = slice(128 * p, 128 * p + 128)
        lo = low_half((BLOCK, 128))
        lo1 = low_half((1, 128))
        g = pre[:, lanes]
        sg = sigmoid(g)
        silu = g * sg
        y = mixed[:, lanes]
        gated = y * silu
        ng = ngrad[:, lanes]
        gn = gain[:, lanes]
        gi = gated * inv
        normed[:, lanes] = (gi * gn).astype(bf16)
        g_gain[:, lanes] += jnp.sum(ng * gi, axis=0, keepdims=True)
        gg = inv * (ng * gn) - gated * pull
        own[:, lanes] = (gg * y * (sg * (1.0 + g * (1.0 - sg)))).astype(bf16)
        dy = gg * silu
        cx = conv(128 * p, 128)
        sx = sigmoid(cx)
        x = (cx * sx).astype(bf16)
        xf = x.astype(f32)
        dyh = dy.astype(bf16)
        zero = jnp.zeros_like(x)
        xs = [jnp.where(lo, x, zero), jnp.where(lo, zero, x)]
        dys = [jnp.where(lo, dyh, zero), jnp.where(lo, zero, dyh)]
        tops, bottoms = [], []
        for i in range(2):
            h = 2 * p + i
            w_top = jnp.exp2(jnp.minimum(ldrow[h : h + 1, :] + rcol[:half, h : h + 1], 40.0))
            s_top = scr[:half, :]
            m_top = w_top * s_top
            tops.append(mm(m_top.astype(bf16), dys[i], NN))
            gm = mm(xs[i][:half], dyh, NT) * w_top
            acc[:half, :] += gm
            e_top = gm * s_top
            w_bot = jnp.exp2(jnp.minimum(ldrow[h : h + 1, half:] + rcol[half:, h : h + 1], 40.0))
            s_bot = scr[half:, half:]
            m_bot = w_bot * s_bot
            bottoms.append(mm(m_bot.astype(bf16), dys[i][half:], NN))
            gm = mm(xs[i][half:], dyh[half:], NT) * w_bot
            acc[half:, half:] += gm
            e_bot = gm * s_bot
            cold[:half, h : h + 1] = jnp.sum(e_top, axis=1, keepdims=True)
            cold[half:, h : h + 1] = jnp.sum(e_bot, axis=1, keepdims=True)
            top_row = jnp.sum(e_top, axis=0, keepdims=True)
            rowd[h : h + 1, :half] = top_row[:, :half]
            rowd[h : h + 1, half:] = top_row[:, half:] + jnp.sum(e_bot, axis=0, keepdims=True)
        dxm = jnp.concatenate([tops[0] + tops[1], bottoms[0] + bottoms[1]], axis=0)
        ds = carry[:, lanes]
        dsh = ds.astype(bf16)
        s_in = jnp.where(k == 0, 0.0, s_in_ref[0, :, lanes])
        s_h = s_in.astype(bf16)
        e_pair = pair_of(eld, p)
        t_pair = pair_of(tail, p)
        dye = (dy * e_pair).astype(bf16)
        cross = mm(c, s_h, NN) * e_pair * dy
        w = mm(b, dsh, NN) * t_pair
        wx = w * xf
        for i in range(2):
            h = 2 * p + i
            keep = lo if i == 0 else jnp.logical_not(lo)
            xw[:, h : h + 1] = jnp.sum(jnp.where(keep, wx, 0.0), axis=1, keepdims=True)
            xw[:, 64 + h : 65 + h] = jnp.sum(jnp.where(keep, cross, 0.0), axis=1, keepdims=True)
        d_c = d_c + mm(dye, s_h, NT)
        d_b = d_b + mm((xf * t_pair).astype(bf16), dsh, NT)
        skip_pair = pair_of(heads3[2:3, :heads], p)
        dx = dxm + skip_pair * dy + w
        dskip = jnp.sum(dy * xf, axis=0, keepdims=True)
        dstate = jnp.sum(ds * s_in, axis=0, keepdims=True) * e_pair[BLOCK - 1 :, :]
        for i in range(2):
            h = 2 * p + i
            keep = lo1 if i == 0 else jnp.logical_not(lo1)
            skips = jnp.where(head_lane == h, jnp.sum(jnp.where(keep, dskip, 0.0), axis=1, keepdims=True), skips)
            carried = jnp.where(head_lane == h, jnp.sum(jnp.where(keep, dstate, 0.0), axis=1, keepdims=True), carried)
        carry[:, lanes] = e_pair[BLOCK - 1 :, :] * ds + mm(c, dye, TN)
        dext[:BLOCK, lanes] = dx * (sx * (1.0 + cx * (1.0 - sx)))
    ah = jnp.where(triangle(True, upper=True), acc[...], 0.0).astype(bf16)
    d_b = d_b + mm(ah, c, NN)
    d_c = d_c + mm(ah, b, TN)
    dext[:BLOCK, inner : inner + nst] = d_b * dsilu(cb)
    dext[:BLOCK, inner + nst :] = d_c * dsilu(cc)
    colsum = cold[...]
    rowsum = jnp.transpose(jnp.concatenate([rowd[...], jnp.zeros((128 - heads, BLOCK), f32)], axis=0))
    xwv = xw[...]
    crossv = pltpu.roll(xwv, 64, 1)
    lane = lax.broadcasted_iota(jnp.int32, (BLOCK, 128), 1)
    tailv = jnp.where(lane < heads, xwv, 0.0)
    crossv = jnp.where(lane < heads, crossv, 0.0)
    upper = triangle(True, upper=True).astype(f32)
    strict = triangle(False).astype(f32)
    from_q = mm(upper, rowsum - colsum + crossv, NN, highest) + mm(strict, tailv, NN, highest) + carried
    ddec = -from_q[:, :heads]
    q = (colsum + tailv)[:, :heads]
    sz = sigmoid(z)
    ratio = jnp.where(step > 1e-30, sz / jnp.where(step > 1e-30, step, 1.0), 1.0)
    dz = q * ratio + rate * ddec * sz
    own[:, a_step : a_step + heads] = dz.astype(bf16)
    g_heads[0:1, :heads] += jnp.sum(dz, axis=0, keepdims=True)
    g_heads[1:2, :heads] += rate * jnp.sum(step * ddec, axis=0, keepdims=True)
    g_heads[2:3, :] += skips
    for at in range(0, inner + state, 256):
        lanes = slice(at, at + 256)
        dpre = taps[3:4, lanes] * dext[0:BLOCK, lanes]
        for j in range(3):
            dpre = dpre + taps[j : j + 1, lanes] * dext[3 - j : 3 - j + BLOCK, lanes]
        own[:, inner + at : inner + at + 256] = dpre.astype(bf16)
        d = dext[0:BLOCK, lanes]
        for j in range(4):
            g_taps[j : j + 1, lanes] += jnp.sum(d * ext[HALO - 3 + j : HALO - 3 + j + BLOCK, lanes], axis=0, keepdims=True)
    dext[BLOCK:, :] = dext[0:HALO, :]


def mix_backward(pre, mixed, ngrad, rows2, states, taps, heads3, gain, inner, state, heads):
    rows = pre.shape[0]
    blocks = rows // BLOCK
    width = pre.shape[1]
    nst = state // 2
    last = blocks - 1
    per = BLOCK // HALO
    return pl.pallas_call(
        functools.partial(bwd_kernel, (inner, state, heads)),
        grid=(blocks,),
        in_specs=[
            pl.BlockSpec((BLOCK, width), lambda k: (last - k, 0)),
            pl.BlockSpec((HALO, width), lambda k: (jnp.maximum((last - k) * per - 1, 0), 0)),
            pl.BlockSpec((BLOCK, inner), lambda k: (last - k, 0)),
            pl.BlockSpec((BLOCK, inner), lambda k: (last - k, 0)),
            pl.BlockSpec((BLOCK, 2), lambda k: (last - k, 0)),
            pl.BlockSpec((1, nst, inner), lambda k: (jnp.maximum(last - k - 1, 0), 0, 0)),
            pl.BlockSpec((4, inner + state), lambda k: (0, 0)),
            pl.BlockSpec((3, heads), lambda k: (0, 0)),
            pl.BlockSpec((1, inner), lambda k: (0, 0)),
        ],
        out_specs=[
            pl.BlockSpec((BLOCK, width), lambda k: (last - k, 0)),
            pl.BlockSpec((BLOCK, inner), lambda k: (last - k, 0)),
            pl.BlockSpec((4, inner + state), lambda k: (0, 0)),
            pl.BlockSpec((8, 128), lambda k: (0, 0)),
            pl.BlockSpec((1, inner), lambda k: (0, 0)),
        ],
        out_shape=[
            jax.ShapeDtypeStruct((rows, width), bf16),
            jax.ShapeDtypeStruct((rows, inner), bf16),
            jax.ShapeDtypeStruct((4, inner + state), f32),
            jax.ShapeDtypeStruct((8, 128), f32),
            jax.ShapeDtypeStruct((1, inner), f32),
        ],
        scratch_shapes=[
            pltpu.VMEM((BLOCK + HALO, inner + state), f32),
            pltpu.VMEM((BLOCK + HALO, inner + state), f32),
            pltpu.VMEM((nst, inner), f32),
            pltpu.VMEM((BLOCK, BLOCK), f32),
            pltpu.VMEM((BLOCK, BLOCK), f32),
            pltpu.VMEM((8, 128), f32),
            pltpu.VMEM((8, 128), f32),
            pltpu.VMEM((BLOCK, 128), f32),
            pltpu.VMEM((heads, BLOCK), f32),
            pltpu.VMEM((BLOCK, 128), f32),
        ],
        name="mix_backward",
    )(pre, pre, mixed, ngrad, rows2, states, taps, heads3, gain)


def on_device(
    block_input,
    out_grad,
    lengths,
    norm_gain,
    in_weight,
    state_weight,
    step_weight,
    conv_inner,
    conv_state,
    step_bias,
    decay_log,
    skip_gain,
    gate_gain,
    out_weight,
):
    sections = lax.axis_size("section")
    section_id = lax.axis_index("section")
    dp_count = lax.axis_size("dp")
    dp_index = lax.axis_index("dp")
    part_count = lax.axis_size("mp")
    part_index = lax.axis_index("mp")
    row_count, model_width = block_input.shape[2:]
    inner_local = in_weight.shape[3]
    inner_total = inner_local * part_count
    state_width = state_weight.shape[2]
    heads_local = step_weight.shape[2]
    first = section_id == 0
    swap = [(0, 1), (1, 0)]

    rows_in = lax.dynamic_index_in_dim(block_input[:, 0], section_id, 0, keepdims=False)
    outer_grad = lax.dynamic_index_in_dim(out_grad[:, 0], section_id, 0, keepdims=False)
    live = lax.dynamic_index_in_dim(lengths[:, 0], section_id, 0, keepdims=False)
    positions = part_index * row_count + jnp.arange(row_count, dtype=jnp.int32)
    mask = (positions < live).astype(f32)[:, None]

    small_shapes = [norm_gain.shape, conv_inner.shape, conv_state.shape, step_bias.shape, decay_log.shape, skip_gain.shape, gate_gain.shape]
    packed = jnp.concatenate([v.reshape(-1) for v in (norm_gain, conv_inner, conv_state, step_bias, decay_log, skip_gain, gate_gain)])
    packed = lax.all_gather(packed, "section")
    smalls = []
    for layer in range(sections):
        at, pieces = 0, []
        for shape in small_shapes:
            size = 1
            for s in shape:
                size *= s
            pieces.append(packed[layer, at : at + size].reshape(shape[1:]))
            at += size
        smalls.append(
            (
                pieces[0],
                jnp.concatenate([pieces[1], pieces[2]], axis=1),
                jnp.stack(pieces[3:6]),
                pieces[6].reshape(1, -1),
            )
        )

    def other_section(weight):
        quarter = weight.shape[0] // dp_count
        mine = lax.dynamic_slice_in_dim(weight, dp_index * quarter, quarter, 0)
        theirs = lax.ppermute(mine, "section", swap)
        return lax.all_gather(theirs, "dp", axis=0, tiled=True)

    own_in = jnp.concatenate([in_weight[0, :, 0], in_weight[0, :, 1], state_weight[0], step_weight[0]], axis=1)
    own_out = out_weight[0]
    other_in = other_section(own_in)
    other_out = other_section(own_out)
    weights = [
        (jnp.where(first, own_in, other_in), jnp.where(first, own_out, other_out)),
        (jnp.where(first, other_in, own_in), jnp.where(first, other_out, own_out)),
    ]
    at_inner, at_state, at_step = inner_local, 2 * inner_local, 2 * inner_local + state_width

    def forward(layer, values):
        w_in, w_out = weights[layer]
        gain_norm, taps, heads3, gain_gate = smalls[layer]
        row_scale = lax.rsqrt(jnp.mean(values * values, axis=1, keepdims=True) + epsilon)
        normal = (values * row_scale * gain_norm).astype(bf16)
        gathered = lax.all_gather(normal, "mp", axis=0, tiled=True)
        pre = jnp.dot(gathered, w_in, preferred_element_type=f32)
        mixed, scaled, sq, states = mix_forward(pre, taps, heads3, gain_gate, inner_local, state_width, heads_local)
        squares = lax.psum_scatter(sq[:, 0], "mp", scatter_dimension=0, tiled=True)
        inv_rms = lax.rsqrt(squares / inner_total + epsilon)[:, None]
        part = jnp.dot(scaled, w_out, preferred_element_type=f32).astype(bf16)
        branch = lax.psum_scatter(part, "mp", scatter_dimension=0, tiled=True).astype(f32) * inv_rms
        result = (values + mask * branch).astype(bf16)
        return result, (values, row_scale, gathered, pre, mixed, states, inv_rms, branch)

    def backward(layer, kept, grad):
        w_in, w_out = weights[layer]
        gain_norm, taps, heads3, gain_gate = smalls[layer]
        values, row_scale, gathered, pre, mixed, states, inv_own, branch = kept
        branch_grad = (mask * grad).astype(bf16)
        pull_own = inv_own * inv_own * jnp.sum(branch_grad.astype(f32) * branch, axis=1, keepdims=True) / inner_total
        scalars = lax.all_gather(jnp.concatenate([inv_own, pull_own], axis=1), "mp", axis=0, tiled=True)
        full_grad = lax.all_gather(branch_grad, "mp", axis=0, tiled=True)
        normed_grad = jnp.einsum("ld,id->li", full_grad, w_out, preferred_element_type=f32)
        own_grad, normed, g_taps, g_heads, g_gain = mix_backward(
            pre, mixed, normed_grad, scalars, states, taps, heads3, gain_gate, inner_local, state_width, heads_local
        )
        out_part = jnp.einsum("li,ld->id", normed, full_grad, preferred_element_type=f32)
        in_part = jnp.einsum("ld,lc->dc", gathered, own_grad, preferred_element_type=f32)
        part = jnp.einsum("lc,dc->ld", own_grad, w_in, preferred_element_type=f32).astype(bf16)
        normal_grad = lax.psum_scatter(part, "mp", scatter_dimension=0, tiled=True).astype(f32)
        norm_part = jnp.sum(normal_grad * values * row_scale, axis=0)
        scaled_in = normal_grad * gain_norm
        input_grad = (
            grad
            + row_scale * scaled_in
            - values * row_scale**3 * jnp.mean(scaled_in * values, axis=1, keepdims=True)
        )
        own_small = (g_taps[:, :inner_local], g_heads[0, :heads_local], g_heads[1, :heads_local], g_heads[2, :heads_local], g_gain[0])
        common_small = (norm_part, g_taps[:, inner_local:])
        return input_grad, in_part.astype(bf16), out_part.astype(bf16), own_small, common_small

    def spread(part):
        return lax.psum_scatter(part, "dp", scatter_dimension=0, tiled=True)

    hidden, kept_first = forward(0, rows_in.astype(f32))
    final, kept_second = forward(1, hidden.astype(f32))
    second_grad, in_second, out_second, own_second, common_second = backward(1, kept_second, outer_grad.astype(f32))
    first_grad, in_first, out_first, own_first, common_first = backward(0, kept_first, second_grad.astype(bf16).astype(f32))

    out_second, in_second = spread(out_second), spread(in_second)
    out_first, in_first = spread(out_first), spread(in_first)

    def to_owner(part_first, part_second):
        mine = jnp.where(first, part_first, part_second).astype(f32)
        theirs = jnp.where(first, part_second, part_first)
        total = (mine + lax.ppermute(theirs, "section", swap).astype(f32)).astype(bf16)
        return total

    out_total = lax.all_gather(to_owner(out_first, out_second), "dp", axis=0, tiled=True)
    in_quarter = to_owner(in_first, in_second)
    state_quarter = lax.psum(in_quarter[:, at_state:at_step].astype(f32), "mp").astype(bf16)
    in_total = lax.all_gather(in_quarter, "dp", axis=0, tiled=True)
    state_total = lax.all_gather(state_quarter, "dp", axis=0, tiled=True)

    def flat(pieces):
        return jnp.concatenate([v.reshape(-1) for v in pieces])

    own_sum = lax.psum(jnp.stack([flat(own_first), flat(own_second)]), ("section", "dp"))
    common_sum = lax.psum(jnp.stack([flat(common_first), flat(common_second)]), ("section", "dp", "mp"))
    own_sum = lax.dynamic_index_in_dim(own_sum, section_id, 0, keepdims=False)
    common_sum = lax.dynamic_index_in_dim(common_sum, section_id, 0, keepdims=False)

    def cut(vector, shapes):
        at, pieces = 0, []
        for shape in shapes:
            size = 1
            for s in shape:
                size *= s
            pieces.append(vector[at : at + size].reshape((1,) + tuple(shape)))
            at += size
        return pieces

    g_conv_inner, g_bias, g_decay, g_skip, g_gate_gain = cut(own_sum, [v.shape for v in own_first])
    g_norm, g_conv_state = cut(common_sum, [v.shape for v in common_first])

    def by_section(of_first, of_second):
        mine = jnp.where(first, of_first, of_second)
        theirs = lax.ppermute(jnp.where(first, of_second, of_first).astype(bf16), "section", swap).astype(mine.dtype)
        return jnp.where(first, jnp.stack([mine, theirs]), jnp.stack([theirs, mine]))[None, :, None]

    in_total = in_total.astype(f32)
    return (
        by_section(hidden, final),
        by_section(first_grad, second_grad),
        g_norm,
        jnp.stack([in_total[:, :at_inner], in_total[:, at_inner:at_state]], axis=1)[None],
        state_total.astype(f32)[None],
        in_total[:, at_step:][None],
        g_conv_inner,
        g_conv_state,
        g_bias,
        g_decay,
        g_skip,
        g_gate_gain,
        out_total.astype(f32)[None],
    )


def solution(mesh):
    return jax.shard_map(
        on_device,
        mesh=mesh,
        in_specs=(
            P(None, "dp", "mp", None),
            P(None, "dp", "mp", None),
            P(None, "dp"),
            P("section", None),
            P("section", None, None, "mp"),
            P("section", None, None),
            P("section", None, "mp"),
            P("section", None, "mp"),
            P("section", None, None),
            P("section", "mp"),
            P("section", "mp"),
            P("section", "mp"),
            P("section", "mp"),
            P("section", "mp", None),
        ),
        out_specs=(
            P("section", None, "dp", "mp", None),
            P("section", None, "dp", "mp", None),
            P("section", None),
            P("section", None, None, "mp"),
            P("section", None, None),
            P("section", None, "mp"),
            P("section", None, "mp"),
            P("section", None, None),
            P("section", "mp"),
            P("section", "mp"),
            P("section", "mp"),
            P("section", "mp"),
            P("section", "mp", None),
        ),
        check_vma=False,
    )
```

time: 3270 us -> 1410 us (0.43)
  waiting for transfers between devices: 1590 us -> 764 us
  matrix products: 637 us -> 162 us
  other arithmetic: 322 us -> 77.3 us
  blocking collectives: 381 us -> 169 us
  local copies, waits for them, and re-layouts: 264 us -> 80.4 us
  Pallas kernels: 0 us -> 124 us
  loops' own time: 38.6 us -> 0 us
    dot_general x75 -> x12, matrix products: 626 us -> 162 us  [the longest x2 37.4 us: forward(): pre = jnp.dot(gathered, w_in, preferred_element_type=f32)]
    psum x1 -> x0, waiting for transfers between devices: 399 us -> none  [on_device(): lax.psum((totals[0], totals[1], totals[2], totals[3], totals[4], totals[5...]
    psum x14 -> x3, blocking collectives: 381 us -> 104 us  [the longest x1 40.9 us: on_device(): lax.psum(in_quarter[:, at_state:at_step].astype(f32), 'mp').astype(bf16)]
    reduce_scatter x6 -> x8, waiting for transfers between devices: 582 us -> 331 us  [the longest x2 129 us: forward(): lax.psum_scatter(part, 'mp', scatter_dimension=0, tiled=True).astype(f32)]
    all_gather x9, waiting for transfers between devices: 473 us -> 241 us  [the longest x2 120 us: backward(): full_grad = lax.all_gather(branch_grad, 'mp', axis=0, tiled=True)]
    pallas_call x0 -> x4, Pallas kernels: none -> 124 us  [the longest x2 83.3 us: mix_backward(): pl.pallas_call(functools.partial(bwd_kernel, (inner, state, heads)), grid...]
    reduce_sum x39 -> x6, other arithmetic: 111 us -> 13.4 us  [the longest x2 6.27 us: backward(): jnp.sum(branch_grad.astype(f32) * branch, axis=1, keepdims=True)]
    while x694 -> x0, local copies, waits for them, and re-layouts: 72.6 us -> none
  transfers between devices with their start and end apart: 22 -> 24, of which waited for: 19 -> 15; matrix products, arithmetic and copies ran while one was open for 12% -> 13% of each run, Pallas kernels for 0% -> 4%
where the time goes in v1:
time: 1410 us; the launch traced here: 1400 us
  waiting for transfers between devices  764 us (54%)
  blocking collectives  169 us (12%)
  matrix products  162 us (11%)
  Pallas kernels  124 us (9%)
  local copies, waits for them, and re-layouts  80.4 us (6%)
  other arithmetic  77.3 us (5%)
  between operations  16.7 us (1%)
    reduce_scatter x2, waiting for transfers between devices, forward(): lax.psum_scatter(part, 'mp', scatter_dimension=0, tiled=True).astype(f32)  129 us
    reduce_scatter x4, waiting for transfers between devices, spread(): return lax.psum_scatter(part, 'dp', scatter_dimension=0, tiled=True)  127 us
    all_gather x2, waiting for transfers between devices, backward(): full_grad = lax.all_gather(branch_grad, 'mp', axis=0, tiled=True)  120 us
    pallas_call x2, Pallas kernels, mix_backward(): pl.pallas_call(functools.partial(bwd_kernel, (inner, state, heads)), grid...  83.3 us
    all_gather x2, waiting for transfers between devices, forward(): gathered = lax.all_gather(normal, 'mp', axis=0, tiled=True)  80.7 us
    reduce_scatter x2, waiting for transfers between devices, backward(): lax.psum_scatter(part, 'mp', scatter_dimension=0, tiled=True).astype(f32)  74.9 us
    ppermute x2, waiting for transfers between devices, to_owner(): lax.ppermute(theirs, 'section', swap).astype(f32)  74.8 us
    ppermute x2, waiting for transfers between devices, other_section(): theirs = lax.ppermute(mine, 'section', swap)  74.8 us
  transfers between devices with their start and end apart: 24, of which 15 were waited for; matrix products, arithmetic and copies ran while one was open for 13% of the time, Pallas kernels for 4%

profile of v1, /device:TPU:0, one launch (start us, length us, event | category | flops | bytes accessed | tf_op | source)
XLA Modules:
  0.0 1404.2 jit_solution(16824576046054707941)
XLA Ops:
  15.9 19.8 %all-reduce.6.cloned.1.call-done = f32[16480]{0:T(1024)} async-done(((f32[16480]{0:T(1024)}), f32[16480]{0:T(1024)}) %all-reduce.6.cloned.1.call-update) | async-done | bytes 65936
  39.3 16.6 %fusion.40 = (bf16[1,2048,1,1024]{3,2,1,0:T(2,128)(2,1)S(1)}, bf16[1,2048,1,1024]{3,2,1,0:T(2,128)(2,1)S(1)}) fusion(bf16[1,2048,2,1024]{3,2,1,0:T(2,128)(2,1)} %param.18), kind=kLoop, calls=%fused_computation.134 | loop fusion | bytes 16777216 | tf_op jit(solution)/shard_map/slice | solution.py:446
  56.0 5.2 copy_bitcast_fusion
  61.2 5.7 pad_maximum_fusion
  70.5 52.2 %collective-permute-done = bf16[512,2320]{0,1:T(8,128)(2,1)S(1)} collective-permute-done((bf16[512,2320]{0,1:T(8,128)(2,1)}, bf16[512,2320]{0,1:T(8,128)(2,1)S(1)}, u32[]{:S(2)}, u32[]{:S(2)}) %collective-permute-start) | collective-permute-done | bytes 2375712 | tf_op jit(solution)/shard_map/ppermute | solution.py:443
  127.9 22.6 %collective-permute-done.1 = bf16[256,2048]{1,0:T(8,128)(2,1)S(1)} collective-permute-done((bf16[256,2048]{1,0:T(8,128)(2,1)S(1)}, bf16[256,2048]{1,0:T(8,128)(2,1)S(1)}, u32[]{:S(2)}, u32[]{:S(2)}) %collective-permute-start.1) | collective-permute-done | bytes 1048608 | tf_op jit(solution)/shard_map/ppermute | solution.py:443
  153.3 40.2 %all-gather.13.cloned.1.call-done = bf16[2048,2320]{1,0:T(8,128)(2,1)} async-done(((bf16[512,2320]{1,0:T(8,128)(2,1)}), bf16[2048,2320]{1,0:T(8,128)(2,1)}) %all-gather.13.cloned.1.call-update) | async-done | bytes 9502736 | tf_op jit(solution)/shard_map/all_gather | solution.py:444
  193.5 17.9 %fusion.1.pre.halo = f32[1024,2320]{1,0:T(8,128)} fusion(bf16[1024,2048]{1,0:T(8,128)(2,1)} %all-gather.11.cloned.1.call-done, bf16[2048,2320]{1,0:T(8,128)(2,1)} %all-gather.13.cloned.1.call-done, pred[]{:T(512)S(6)} %eq.3, bf16[2048,16]{1,0:T(8,128)(2,1)S(1)} %bitcast.131, bf16[2048,256]{1,0:T(8,128)(2,1)S(1)} %bitcast.138, ...), kind=kOutput, calls=%fused_computation.28 | convolution fusion | flops 9773547520 | bytes 32702464 | tf_op jit(solution)/shard_map/dot_general | solution.py:462
  211.4 20.5 %mix_forward.2 = (f32[1024,1024]{1,0:T(8,128)}, bf16[1024,1024]{1,0:T(8,128)(2,1)}, f32[1024,1]{1,0:T(8,128)}, f32[4,128,1024]{2,1,0:T(8,128)}) custom-call(f32[1024,2320]{1,0:T(8,128)} %fusion.1.pre.halo, f32[4,1280]{1,0:T(4,128)} %copy-done.18, f32[3,16]{1,0:T(4,128)} %pad_maximum_fusion.5.heads3, f32[1,1024]{1,0:T(1,128)} %get-tuple-element.119.gain), custom_call_target="tpu_custom_call" | custom-call | tf_op jit(solution)/shard_map/mix_forward/pallas_call | solution.py:137
  232.0 9.3 convolution_convert_fusion.5
  244.1 11.9 all-reduce.1
  256.1 64.9 %reduce-scatter.9.cloned.1.call-done = bf16[256,2048]{1,0:T(8,128)(2,1)} async-done(((bf16[1024,2048]{1,0:T(8,128)(2,1)}), bf16[256,2048]{1,0:T(8,128)(2,1)}) %reduce-scatter.9.cloned.1.call-update) | async-done | bytes 1048592 | tf_op jit(solution)/shard_map/reduce_scatter | solution.py:467
  324.9 80.7 %all-gather.17.cloned.1.call-done = bf16[1024,2048]{1,0:T(8,128)(2,1)} async-done(((bf16[256,2048]{1,0:T(8,128)(2,1)}), bf16[1024,2048]{1,0:T(8,128)(2,1)}) %all-gather.17.cloned.1.call-update) | async-done | bytes 4194320 | tf_op jit(solution)/shard_map/all_gather | solution.py:461
  405.6 19.5 %fusion.3.pre.halo = f32[1024,2320]{1,0:T(8,128)} fusion(bf16[1024,2048]{1,0:T(8,128)(2,1)} %all-gather.17.cloned.1.call-done, bf16[2048,2320]{1,0:T(8,128)(2,1)} %all-gather.13.cloned.1.call-done, pred[]{:T(512)S(6)} %eq.3, bf16[2048,16]{1,0:T(8,128)(2,1)} %bitcast.132, bf16[2048,256]{1,0:T(8,128)(2,1)} %bitcast.135, bf16[2048,1024]{1,0:T(8,128)(2,1)} %copy-done.2, ...), kind=kOutput, calls=%fused_computation.30 | convolution fusion | flops 9773547520 | bytes 32702464 | tf_op jit(solution)/shard_map/dot_general | solution.py:462
  425.2 20.6 %mix_forward.3 = (f32[1024,1024]{1,0:T(8,128)}, bf16[1024,1024]{1,0:T(8,128)(2,1)}, f32[1024,1]{1,0:T(8,128)}, f32[4,128,1024]{2,1,0:T(8,128)}) custom-call(f32[1024,2320]{1,0:T(8,128)} %fusion.3.pre.halo, f32[4,1280]{1,0:T(4,128)} %copy-done.19, f32[3,16]{1,0:T(4,128)} %pad_maximum_fusion.6.heads3, f32[1,1024]{1,0:T(1,128)} %get-tuple-element.110.gain), custom_call_target="tpu_custom_call" | custom-call | tf_op jit(solution)/shard_map/mix_forward/pallas_call | solution.py:137
  445.8 10.6 convolution_convert_fusion.4
  457.8 9.3 all-reduce.2
  467.2 63.9 %reduce-scatter.11.cloned.1.call-done = bf16[256,2048]{1,0:T(8,128)(2,1)} async-done(((bf16[1024,2048]{1,0:T(8,128)(2,1)}), bf16[256,2048]{1,0:T(8,128)(2,1)}) %reduce-scatter.11.cloned.1.call-update) | async-done | bytes 1048592 | tf_op jit(solution)/shard_map/reduce_scatter | solution.py:467
  534.1 18.9 %all_gather.46.rows2 = f32[1024,2]{1,0:T(8,128)} all-gather(f32[256,2]{1,0:T(8,128)S(1)} %copy.59), channel_id=1, replica_groups=mesh['section'=2,'dp'=4,'mp'=4] {'mp'}, dimensions={0}, use_global_device_ids=true | all-gather | bytes 10240 | tf_op jit(solution)/shard_map/all_gather | solution.py:477
  553.1 64.1 %all-gather.19.cloned.1.call-done = bf16[1024,2048]{1,0:T(8,128)(2,1)} async-done(((bf16[256,2048]{1,0:T(8,128)(2,1)}), bf16[1024,2048]{1,0:T(8,128)(2,1)}) %all-gather.19.cloned.1.call-update) | async-done | bytes 4194320 | tf_op jit(solution)/shard_map/all_gather | solution.py:478
  617.2 11.2 fusion.29.ngrad
  628.4 41.5 %mix_backward.2 = (bf16[1024,2320]{1,0:T(8,128)(2,1)}, bf16[1024,1024]{1,0:T(8,128)(2,1)}, f32[4,1280]{1,0:T(4,128)}, f32[8,128]{1,0:T(8,128)}, f32[1,1024]{1,0:T(1,128)}) custom-call(f32[1024,2320]{1,0:T(8,128)} %fusion.3.pre.halo, f32[1024,2320]{1,0:T(8,128)} %fusion.3.pre.halo, f32[1024,1024]{1,0:T(8,128)} %get-tuple-element.35.mixed, ...), custom_call_target="tpu_custom_call" | custom-call | tf_op jit(solution)/shard_map/mix_backward/pallas_call | solution.py:339
  669.9 17.0 %fusion.4 = bf16[1024,2048]{1,0:T(8,128)(2,1)} fusion(bf16[1024,2320]{1,0:T(8,128)(2,1)} %get-tuple-element.37, bf16[2048,2320]{1,0:T(8,128)(2,1)} %all-gather.13.cloned.1.call-done, pred[]{:T(512)S(6)} %eq.3, bf16[2048,16]{1,0:T(8,128)(2,1)} %bitcast.133, bf16[2048,256]{1,0:T(8,128)(2,1)} %bitcast.136, bf16[2048,1024]{1,0:T(8,128)(2,1)} %copy-done.2, ...), kind=kOutput, calls=%fused_computation.35 | convolution fusion | flops 9775644672 | bytes 27951104 | tf_op jit(solution)/shard_map/lc,dc->ld/dot_general | solution.py:485
  687.0 74.8 %reduce-scatter.13.cloned.1.call-done = bf16[256,2048]{1,0:T(8,128)(2,1)} async-done(((bf16[1024,2048]{1,0:T(8,128)(2,1)}), bf16[256,2048]{1,0:T(8,128)(2,1)}) %reduce-scatter.13.cloned.1.call-update) | async-done | bytes 1048592 | tf_op jit(solution)/shard_map/reduce_scatter | solution.py:486
  767.3 9.3 convolution_convert_fusion.2
  777.0 24.1 %all_gather.48.rows2 = f32[1024,2]{1,0:T(8,128)} all-gather(f32[256,2]{1,0:T(8,128)S(1)} %copy.62), channel_id=1, replica_groups=mesh['section'=2,'dp'=4,'mp'=4] {'mp'}, dimensions={0}, use_global_device_ids=true | all-gather | bytes 10240 | tf_op jit(solution)/shard_map/all_gather | solution.py:477
  801.1 55.9 %all-gather.21.cloned.1.call-done = bf16[1024,2048]{1,0:T(8,128)(2,1)} async-done(((bf16[256,2048]{1,0:T(8,128)(2,1)}), bf16[1024,2048]{1,0:T(8,128)(2,1)}) %all-gather.21.cloned.1.call-update) | async-done | bytes 4194320 | tf_op jit(solution)/shard_map/all_gather | solution.py:478
  857.0 10.5 fusion.28.ngrad
  867.5 41.8 %mix_backward.3 = (bf16[1024,2320]{1,0:T(8,128)(2,1)}, bf16[1024,1024]{1,0:T(8,128)(2,1)}, f32[4,1280]{1,0:T(4,128)}, f32[8,128]{1,0:T(8,128)}, f32[1,1024]{1,0:T(1,128)}) custom-call(f32[1024,2320]{1,0:T(8,128)} %fusion.1.pre.halo, f32[1024,2320]{1,0:T(8,128)} %fusion.1.pre.halo, f32[1024,1024]{1,0:T(8,128)} %get-tuple-element.38.mixed, ...), custom_call_target="tpu_custom_call" | custom-call | tf_op jit(solution)/shard_map/mix_backward/pallas_call | solution.py:339
  909.3 9.3 convolution_convert_fusion.3
  918.7 15.5 %convolution_convert_fusion = bf16[2048,2320]{0,1:T(8,128)(2,1)} fusion(bf16[1024,2048]{1,0:T(8,128)(2,1)} %all-gather.17.cloned.1.call-done, bf16[1024,2320]{1,0:T(8,128)(2,1)} %get-tuple-element.37), kind=kOutput, calls=%fused_computation.1 | convolution fusion | flops 9735536640 | bytes 18448384 | tf_op jit(solution)/shard_map/ld,lc->dc/dot_general | solution.py:484
  934.3 16.0 %convolution_convert_fusion.1 = bf16[2048,2320]{0,1:T(8,128)(2,1)} fusion(bf16[1024,2048]{1,0:T(8,128)(2,1)} %all-gather.11.cloned.1.call-done, bf16[1024,2320]{1,0:T(8,128)(2,1)} %get-tuple-element.40), kind=kOutput, calls=%fused_computation.2 | convolution fusion | flops 9735536640 | bytes 18448384 | tf_op jit(solution)/shard_map/ld,lc->dc/dot_general | solution.py:484
  951.7 15.8 %fusion.5 = bf16[1024,2048]{1,0:T(8,128)(2,1)} fusion(bf16[1024,2320]{1,0:T(8,128)(2,1)} %get-tuple-element.40, bf16[2048,2320]{1,0:T(8,128)(2,1)} %all-gather.13.cloned.1.call-done, pred[]{:T(512)S(6)} %eq.3, bf16[2048,16]{1,0:T(8,128)(2,1)S(1)} %bitcast.134, bf16[2048,256]{1,0:T(8,128)(2,1)S(1)} %bitcast.139, bf16[2048,1024]{1,0:T(8,128)(2,1)} %copy-done.2, ...), kind=kOutput, calls=%fused_computation.36 | convolution fusion | flops 9775644672 | bytes 27951104 | tf_op jit(solution)/shard_map/lc,dc->ld/dot_general | solution.py:485
  972.4 23.1 %collective-permute-done.5 = bf16[256,2048]{1,0:T(8,128)(2,1)S(1)} collective-permute-done((bf16[256,2048]{1,0:T(8,128)(2,1)S(1)}, bf16[256,2048]{1,0:T(8,128)(2,1)S(1)}, u32[]{:S(2)}, u32[]{:S(2)}) %collective-permute-start.5) | collective-permute-done | bytes 1048608 | tf_op jit(solution)/shard_map/ppermute | solution.py:512
  998.3 46.3 %reduce-scatter.19.cloned.1.call-done = bf16[512,2320]{0,1:T(8,128)(2,1)} async-done(((bf16[2048,2320]{0,1:T(8,128)(2,1)}), bf16[512,2320]{0,1:T(8,128)(2,1)}) %reduce-scatter.19.cloned.1.call-update) | async-done | bytes 2375696 | tf_op jit(solution)/shard_map/reduce_scatter | solution.py:499
  1044.6 80.7 %reduce-scatter.17.cloned.1.call-done = bf16[512,2320]{0,1:T(8,128)(2,1)} async-done(((bf16[2048,2320]{0,1:T(8,128)(2,1)}), bf16[512,2320]{0,1:T(8,128)(2,1)}) %reduce-scatter.17.cloned.1.call-update) | async-done | bytes 2375696 | tf_op jit(solution)/shard_map/reduce_scatter | solution.py:499
  1128.9 51.7 %collective-permute-done.4 = bf16[512,2320]{0,1:T(8,128)(2,1)S(1)} collective-permute-done((bf16[512,2320]{0,1:T(8,128)(2,1)S(1)}, bf16[512,2320]{0,1:T(8,128)(2,1)S(1)}, u32[]{:S(2)}, u32[]{:S(2)}) %collective-permute-start.4) | collective-permute-done | bytes 2375712 | tf_op jit(solution)/shard_map/ppermute | solution.py:512
  1182.6 40.9 %all-reduce.7 = bf16[512,256]{0,1:T(8,128)(2,1)} all-reduce(f32[512,256]{0,1:T(8,128)} %slice_convert_fusion), channel_id=1, replica_groups=mesh['section'=2,'dp'=4,'mp'=4] {'mp'}, use_global_device_ids=true, to_apply=%region_17.18 | all-reduce | flops 131072 | bytes 786432 | tf_op jit(solution)/shard_map/psum | solution.py:517
  1229.4 22.1 %collective-permute-done.2 = bf16[256,2048]{1,0:T(8,128)(2,1)} collective-permute-done((bf16[256,2048]{1,0:T(8,128)(2,1)}, bf16[256,2048]{1,0:T(8,128)(2,1)}, u32[]{:S(2)}, u32[]{:S(2)}) %collective-permute-start.2) | collective-permute-done | bytes 1048608 | tf_op jit(solution)/shard_map/ppermute | solution.py:544
  1251.4 3.9 maximum_select_fusion.1
  1259.1 5.3 select_bitcast_fusion
  1265.9 23.7 %psum.23 = f32[2,5168]{1,0:T(2,128)S(1)} all-reduce(f32[2,5168]{1,0:T(2,128)S(1)} %pad_maximum_fusion.1), channel_id=1, replica_groups=mesh['section'=2,'dp'=4,'mp'=4] {'section','dp'}, use_global_device_ids=true, to_apply=%region_18.19 | all-reduce | flops 10336 | bytes 82688 | tf_op jit(solution)/shard_map/psum | solution.py:524
  1291.5 39.6 %psum.21 = f32[2,3072]{1,0:T(2,128)S(1)} all-reduce(f32[2,3072]{1,0:T(2,128)S(1)} %pad_maximum_fusion.2), channel_id=1, replica_groups=mesh['section'=2,'dp'=4,'mp'=4] {'section','dp','mp'}, use_global_device_ids=true, to_apply=%region_14.15 | all-reduce | flops 6144 | bytes 49152 | tf_op jit(solution)/shard_map/psum | solution.py:525
  1335.1 6.7 bitcast_convert_fusion
  1345.0 12.6 convert_element_type.151
  1357.6 6.5 slice_bitcast_fusion.1
  1365.7 6.0 maximum_bitcast_fusion
  1371.7 25.3 %copy.65 = f32[1,2048,2,1024]{3,2,1,0:T(2,128)} copy(f32[1,2048,2,1024]{1,3,2,0:T(8,128)} %maximum_bitcast_fusion) | data formatting | bytes 33554432
  (202 shorter events, 76.0 us)
Async XLA Ops:
  7.2 234.2 %copy-start = (s32[2,1]{0,1:T(1,128)S(1)}, s32[2,1]{0,1:T(1,128)}, u32[]{:S(2)}) copy-start(s32[2,1]{0,1:T(1,128)} %param.16) | copy-start | bytes 28
  7.2 28.5 %all-reduce.6.cloned.1.call-start = ((), (), s32[]{:S(2)}) async-start(), calls=%async_computation.25 | async-start | bytes 139264
  12.6 140.6 %all-gather.11.cloned.1.call-start = ((), (), s32[]{:S(2)}) async-start(), calls=%async_computation.8 | async-start | bytes 5242880 | tf_op jit(solution)/shard_map/all_gather | solution.py:461
  14.8 41.2 %copy-start.24 = (f32[256]{0:T(256)}, f32[256]{0:T(256)S(1)}, u32[]{:S(2)}) copy-start(f32[256]{0:T(256)S(1)} %get-tuple-element.130) | copy-start | bytes 3076
  15.9 177.6 %copy-start.10 = (bf16[1,2048,16]{2,1,0:T(8,128)(2,1)}, bf16[1,2048,16]{2,1,0:T(8,128)(2,1)S(1)}, u32[]{:S(2)}) copy-start(bf16[1,2048,16]{2,1,0:T(8,128)(2,1)S(1)} %copy.54) | copy-start | bytes 196612
  36.7 19.2 %copy-start.20 = (f32[1,2048]{1,0:T(1,128)}, f32[1,2048]{1,0:T(1,128)S(1)}, u32[]{:S(2)}) copy-start(f32[1,2048]{1,0:T(1,128)S(1)} %get-tuple-element.118) | copy-start | bytes 24580
  39.3 154.3 %all-gather.13.cloned.1.call-start = ((), (), s32[]{:S(2)}) async-start(), calls=%async_computation.9 | async-start | bytes 12451840 | tf_op jit(solution)/shard_map/all_gather | solution.py:444
  69.6 53.1 %collective-permute-start = (bf16[512,2320]{0,1:T(8,128)(2,1)}, bf16[512,2320]{0,1:T(8,128)(2,1)S(1)}, u32[]{:S(2)}, u32[]{:S(2)}) collective-permute-start(bf16[512,2320]{0,1:T(8,128)(2,1)} %copy.55), channel_id=1, source_target_pairs={{0,16},{16,0},{1,17},{17,1},{2,18},{18,2},{3,19},{19,3},{4,20},{20... | collective-permute-start | bytes 7127048 | tf_op jit(solution)/shard_map/ppermute | solution.py:443
  125.4 68.1 %copy-start.13 = (bf16[1,2048,256]{2,1,0:T(8,128)(2,1)S(1)}, bf16[1,2048,256]{2,1,0:T(8,128)(2,1)}, u32[]{:S(2)}) copy-start(bf16[1,2048,256]{2,1,0:T(8,128)(2,1)} %param.19) | copy-start | bytes 3145732
  125.4 106.5 %all-gather.15.cloned.1.call-start = ((), (), s32[]{:S(2)}) async-start(), calls=%async_computation.10 | async-start | bytes 5242880 | tf_op jit(solution)/shard_map/all_gather | solution.py:444
  126.9 23.7 %collective-permute-start.1 = (bf16[256,2048]{1,0:T(8,128)(2,1)S(1)}, bf16[256,2048]{1,0:T(8,128)(2,1)S(1)}, u32[]{:S(2)}, u32[]{:S(2)}) collective-permute-start(bf16[256,2048]{1,0:T(8,128)(2,1)S(1)} %dynamic-slice_bitcast_fusion), channel_id=1, source_target_pairs={{0,16},{16,0},{1,17},{17,1},{2,18},{18,2},{3,19},{19,3},{4,20},{20... | collective-permute-start | bytes 3145736 | tf_op jit(solution)/shard_map/ppermute | solution.py:443
  151.6 169.5 %reduce-scatter.9.cloned.1.call-start = ((), (), s32[]{:S(2)}) async-start(), calls=%async_computation.11 | async-start | bytes 5242880 | tf_op jit(solution)/shard_map/reduce_scatter | solution.py:467
  153.3 58.1 %copy-start.18 = (f32[4,1280]{1,0:T(4,128)}, f32[4,1280]{1,0:T(4,128)S(1)}, u32[]{:S(2)}) copy-start(f32[4,1280]{1,0:T(4,128)S(1)} %constant_dynamic-update-slice_fusion.taps) | copy-start | bytes 61444
  241.3 79.7 %copy-start.3 = (bf16[2,1,256,2048]{3,2,1,0:T(8,128)(2,1)S(1)}, bf16[2,1,256,2048]{3,2,1,0:T(8,128)(2,1)}, u32[]{:S(2)}) copy-start(bf16[2,1,256,2048]{3,2,1,0:T(8,128)(2,1)} %param.14) | copy-start | bytes 6291460
  241.3 164.3 %all-gather.17.cloned.1.call-start = ((), (), s32[]{:S(2)}) async-start(), calls=%async_computation.12 | async-start | bytes 5242880 | tf_op jit(solution)/shard_map/all_gather | solution.py:461
  324.2 206.9 %reduce-scatter.11.cloned.1.call-start = ((), (), s32[]{:S(2)}) async-start(), calls=%async_computation.13 | async-start | bytes 5242880 | tf_op jit(solution)/shard_map/reduce_scatter | solution.py:467
  324.9 100.2 %copy-start.19 = (f32[4,1280]{1,0:T(4,128)}, f32[4,1280]{1,0:T(4,128)S(1)}, u32[]{:S(2)}) copy-start(f32[4,1280]{1,0:T(4,128)S(1)} %constant_dynamic-update-slice_fusion.2.taps) | copy-start | bytes 61444
  456.4 74.7 %copy-start.9 = (bf16[2,1,256,2048]{3,2,1,0:T(8,128)(2,1)S(1)}, bf16[2,1,256,2048]{3,2,1,0:T(8,128)(2,1)}, u32[]{:S(2)}) copy-start(bf16[2,1,256,2048]{3,2,1,0:T(8,128)(2,1)} %param.15) | copy-start | bytes 6291460
  456.4 160.8 %all-gather.19.cloned.1.call-start = ((), (), s32[]{:S(2)}) async-start(), calls=%async_computation.14 | async-start | bytes 5242880 | tf_op jit(solution)/shard_map/all_gather | solution.py:478
  467.2 161.2 %copy-start.26 = (f32[256]{0:T(256)}, f32[256]{0:T(256)S(1)}, u32[]{:S(2)}) copy-start(f32[256]{0:T(256)S(1)} %fusion.34) | copy-start | bytes 3076
  533.8 228.0 %reduce-scatter.13.cloned.1.call-start = ((), (), s32[]{:S(2)}) async-start(), calls=%async_computation.15 | async-start | bytes 5242880 | tf_op jit(solution)/shard_map/reduce_scatter | solution.py:486
  686.9 170.1 %all-gather.21.cloned.1.call-start = ((), (), s32[]{:S(2)}) async-start(), calls=%async_computation.16 | async-start | bytes 5242880 | tf_op jit(solution)/shard_map/all_gather | solution.py:478
  767.3 200.3 %reduce-scatter.23.cloned.1.call-start = ((), (), s32[]{:S(2)}) async-start(), calls=%async_computation.23 | async-start | bytes 5242880 | tf_op jit(solution)/shard_map/reduce_scatter | solution.py:499
  776.7 190.9 %reduce-scatter.21.cloned.1.call-start = ((), (), s32[]{:S(2)}) async-start(), calls=%async_computation.22 | async-start | bytes 5242880 | tf_op jit(solution)/shard_map/reduce_scatter | solution.py:499
  918.6 126.0 %reduce-scatter.19.cloned.1.call-start = ((), (), s32[]{:S(2)}) async-start(), calls=%async_computation.19 | async-start | bytes 11878400 | tf_op jit(solution)/shard_map/reduce_scatter | solution.py:499
  934.2 191.1 %reduce-scatter.17.cloned.1.call-start = ((), (), s32[]{:S(2)}) async-start(), calls=%async_computation.18 | async-start | bytes 11878400 | tf_op jit(solution)/shard_map/reduce_scatter | solution.py:499
  950.3 306.9 %reduce-scatter.15.cloned.1.call-start = ((), (), s32[]{:S(2)}) async-start(), calls=%async_computation.17 | async-start | bytes 5242880 | tf_op jit(solution)/shard_map/reduce_scatter | solution.py:486
  967.5 367.6 %all-gather.27.cloned.1.call-start = ((), (), s32[]{:S(2)}) async-start(), calls=%async_computation.24 | async-start | bytes 5242880 | tf_op jit(solution)/shard_map/all_gather | solution.py:515
  969.0 26.5 %collective-permute-start.5 = (bf16[256,2048]{1,0:T(8,128)(2,1)S(1)}, bf16[256,2048]{1,0:T(8,128)(2,1)S(1)}, u32[]{:S(2)}, u32[]{:S(2)}) collective-permute-start(bf16[256,2048]{1,0:T(8,128)(2,1)S(1)} %broadcast_select_fusion.11), channel_id=1, source_target_pairs={{0,16},{16,0},{1,17},{17,1},{2,18},{18,2},{3,19},{19,3},{4,20},{20... | collective-permute-start | bytes 3145736 | tf_op jit(solution)/shard_map/ppermute | solution.py:512
  998.3 343.5 %all-gather.25.cloned.1.call-start = ((), (), s32[]{:S(2)}) async-start(), calls=%async_computation.21 | async-start | bytes 1310720 | tf_op jit(solution)/shard_map/all_gather | solution.py:519
  1125.3 55.3 %copy-start.6 = (bf16[512,2320]{0,1:T(8,128)(2,1)S(1)}, bf16[512,2320]{0,1:T(8,128)(2,1)}, u32[]{:S(2)}) copy-start(bf16[512,2320]{0,1:T(8,128)(2,1)} %reduce-scatter.19.cloned.1.call-done) | copy-start | bytes 7127044
  1125.3 55.3 %copy-start.7 = (bf16[512,2320]{0,1:T(8,128)(2,1)S(1)}, bf16[512,2320]{0,1:T(8,128)(2,1)}, u32[]{:S(2)}) copy-start(bf16[512,2320]{0,1:T(8,128)(2,1)} %reduce-scatter.17.cloned.1.call-done) | copy-start | bytes 7127044
  1127.4 53.2 %collective-permute-start.4 = (bf16[512,2320]{0,1:T(8,128)(2,1)S(1)}, bf16[512,2320]{0,1:T(8,128)(2,1)S(1)}, u32[]{:S(2)}, u32[]{:S(2)}) collective-permute-start(bf16[512,2320]{0,1:T(8,128)(2,1)S(1)} %broadcast_select_fusion.10), channel_id=1, source_target_pairs={{0,16},{16,0},{1,17},{17,1},{2,18},{18,2},{3,19},{19,3},{4,20},{20... | collective-permute-start | bytes 7127048 | tf_op jit(solution)/shard_map/ppermute | solution.py:512
  1181.6 42.3 %copy-start.5 = (bf16[512,2320]{0,1:T(8,128)(2,1)}, bf16[512,2320]{0,1:T(8,128)(2,1)S(1)}, u32[]{:S(2)}) copy-start(bf16[512,2320]{0,1:T(8,128)(2,1)S(1)} %add_convert_fusion) | copy-start | bytes 7127044
  1181.6 42.6 %copy-start.27 = (f32[256]{0:T(256)S(1)}, f32[256]{0:T(256)}, u32[]{:S(2)}) copy-start(f32[256]{0:T(256)} %copy-done.26) | copy-start | bytes 3076
  1223.6 121.4 %all-gather.23.cloned.1.call-start = ((), (), s32[]{:S(2)}) async-start(), calls=%async_computation.20 | async-start | bytes 11878400 | tf_op jit(solution)/shard_map/all_gather | solution.py:518
  1224.2 31.1 %copy-start.22 = (f32[4,1280]{1,0:T(4,128)S(1)}, f32[4,1280]{1,0:T(4,128)}, u32[]{:S(2)}) copy-start(f32[4,1280]{1,0:T(4,128)} %get-tuple-element.42) | copy-start | bytes 61444
  1224.2 32.0 %copy-start.29 = (f32[1,1024]{1,0:T(1,128)S(1)}, f32[1,1024]{1,0:T(1,128)}, u32[]{:S(2)}) copy-start(f32[1,1024]{1,0:T(1,128)} %get-tuple-element.46) | copy-start | bytes 12292
  1224.2 32.1 %copy-start.23 = (f32[4,1280]{1,0:T(4,128)S(1)}, f32[4,1280]{1,0:T(4,128)}, u32[]{:S(2)}) copy-start(f32[4,1280]{1,0:T(4,128)} %get-tuple-element.41) | copy-start | bytes 61444
  1224.2 32.9 %copy-start.30 = (f32[1,1024]{1,0:T(1,128)S(1)}, f32[1,1024]{1,0:T(1,128)}, u32[]{:S(2)}) copy-start(f32[1,1024]{1,0:T(1,128)} %get-tuple-element.44) | copy-start | bytes 12292
  1224.2 33.0 %copy-start.4 = (bf16[2,1,256,2048]{3,2,1,0:T(8,128)(2,1)S(1)}, bf16[2,1,256,2048]{3,2,1,0:T(8,128)(2,1)}, u32[]{:S(2)}) copy-start(bf16[2,1,256,2048]{3,2,1,0:T(8,128)(2,1)} %param.14) | copy-start | bytes 6291460
  1224.2 33.0 %copy-start.21 = (f32[1,2048]{1,0:T(1,128)S(1)}, f32[1,2048]{1,0:T(1,128)}, u32[]{:S(2)}) copy-start(f32[1,2048]{1,0:T(1,128)} %copy-done.20) | copy-start | bytes 24580
  1224.2 33.0 %copy-start.25 = (f32[256]{0:T(256)S(1)}, f32[256]{0:T(256)}, u32[]{:S(2)}) copy-start(f32[256]{0:T(256)} %copy-done.24) | copy-start | bytes 3076
  1227.7 31.5 %copy-start.28 = (f32[256]{0:T(256)S(1)}, f32[256]{0:T(256)}, u32[]{:S(2)}) copy-start(f32[256]{0:T(256)} %get-tuple-element.129) | copy-start | bytes 3076
  1227.7 23.8 %collective-permute-start.2 = (bf16[256,2048]{1,0:T(8,128)(2,1)}, bf16[256,2048]{1,0:T(8,128)(2,1)}, u32[]{:S(2)}, u32[]{:S(2)}) collective-permute-start(bf16[256,2048]{1,0:T(8,128)(2,1)} %get-tuple-element.109), channel_id=1, source_target_pairs={{0,16},{16,0},{1,17},{17,1},{2,18},{18,2},{3,19},{19,3},{4,20},{20... | collective-permute-start | bytes 3145736 | tf_op jit(solution)/shard_map/ppermute | solution.py:544
  1264.4 68.4 %copy-start.8 = (f32[1,1,1,256,2048]{4,3,2,1,0:T(8,128)S(1)}, f32[1,1,1,256,2048]{4,3,2,1,0:T(8,128)}, u32[]{:S(2)}) copy-start(f32[1,1,1,256,2048]{4,3,2,1,0:T(8,128)} %get-tuple-element.106) | copy-start | bytes 6291460
  1264.4 68.1 %collective-permute-start.3 = (bf16[256,2048]{1,0:T(8,128)(2,1)}, bf16[256,2048]{1,0:T(8,128)(2,1)S(1)}, u32[]{:S(2)}, u32[]{:S(2)}) collective-permute-start(bf16[256,2048]{1,0:T(8,128)(2,1)} %get-tuple-element.107), channel_id=1, source_target_pairs={{0,16},{16,0},{1,17},{17,1},{2,18},{18,2},{3,19},{19,3},{4,20},{20... | collective-permute-start | bytes 3145736 | tf_op jit(solution)/shard_map/ppermute | solution.py:544
  1371.7 25.3 %copy-start.1 = (s32[2,1]{0,1:T(1,128)S(1)}, s32[2,1]{0,1:T(1,128)}, u32[]{:S(2)}) copy-start(s32[2,1]{0,1:T(1,128)} %param.16) | copy-start | bytes 28
  (8 other events, 18.3 us)
Sparse Core Ops, SparseCore 0:
  12.8 22.8 all-reduce.5
  39.4 81.4 all-gather.10
  125.6 67.8 all-gather.12
  194.9 34.4 all-gather.14
  241.5 79.5 reduce-scatter.8
  324.4 81.2 all-gather.16
  456.5 74.5 reduce-scatter.10
  533.9 83.1 all-gather.18
  687.0 74.7 reduce-scatter.12
  767.4 89.5 all-gather.20
  859.5 43.0 reduce-scatter.22
  918.7 44.4 reduce-scatter.20
  966.4 78.1 reduce-scatter.18
  1047.1 78.1 reduce-scatter.16
  1128.0 87.3 reduce-scatter.14
  1216.8 37.0 all-gather.26
  1255.3 16.8 all-gather.24
  1274.2 66.1 all-gather.22
